TPU v7x, 32 devices: a whole 2x2x4 slice. The times are simulated.
32 devices in a mesh: dp: 4 (over z), row: 8 (over y, x, core).
Axes of the slice: x: 2, y: 2, z: 4, core: 2. Of those that a mesh axis runs over, the one named last changes fastest.
Arguments:
- fields: bfloat16 [4, 16, 512, 2048], P('dp', None, 'row'), may hold values from -6 to 6
- cotangent: bfloat16 [4, 16, 512, 2048], P('dp', None, 'row'), may hold values from -6 to 6
- spectral: bfloat16 [2, 16, 16, 128, 128], P(None, None, None, 'row'), may hold values from -5 to 5
- local_weight: bfloat16 [16, 16], replicated, may hold values from -1.5 to 1.5
- bias: float32 [16], replicated, may hold values from -3 to 3
Outputs:
- field_grad: bfloat16 [4, 16, 512, 2048], P('dp', None, 'row')
- spectral_grad: float32 [2, 16, 16, 128, 128], P(None, None, 'dp', 'row')
- local_grad: float32 [16, 16], replicated
- bias_grad: float32 [16], replicated
All inputs are finite; a program needn't handle non-finite values.
Results may differ from a plain program's by a relative error of at most 0.028.
Values may be sent and summed in bfloat16 or wider, within the bound.
No kernel may reach another device: no remote copies, remote signals or barrier semaphores. Data moves between devices by JAX's collectives and lax.ppermute only.
A program may use at most 128 MiB of HBM per device.

v0:
```python
import functools
import math

import jax
import jax.numpy as jnp
import numpy as np
from jax import lax
from jax.experimental import pallas as pl
from jax.experimental.pallas import tpu as pltpu
from jax.sharding import PartitionSpec as P


BF16 = jnp.bfloat16
F32 = jnp.float32
LANES = 128
TILE = 512
GROUP = 16


def column_table(width, modes):
    turns = np.arange(modes)[:, None] * np.arange(width)[None, :] % width
    angle = np.float32(2.0 * math.pi / width) * turns.astype(np.float32)
    table = np.concatenate([np.cos(angle), -np.sin(angle)], axis=0)
    return table.astype(BF16)


def row_angles(mode, place, height, modes):
    freq = (mode - modes // 2) % height
    turns = freq[:, None] * place[None, :] % height
    return 2.0 * math.pi / height * turns.astype(F32)


def dot(left, right):
    return jnp.dot(left, right, preferred_element_type=F32)


def dot_nt(left, right):
    return lax.dot_general(left, right, (((1,), (1,)), ((), ())), preferred_element_type=F32)


def tree(parts):
    parts = list(parts)
    while len(parts) > 1:
        parts = [parts[at] + parts[at + 1] for at in range(0, len(parts), 2)]
    return parts[0]


def whole(shape):
    return pl.BlockSpec(shape, lambda *_: (0,) * len(shape))


def room(mebibytes):
    return pltpu.CompilerParams(vmem_limit_bytes=mebibytes << 20)


def streamed(value):
    return pltpu.with_memory_space_constraint(value, pltpu.HBM)


def to_pieces(value):
    first = value.astype(BF16).astype(F32)
    rest = value - first
    second = rest.astype(BF16).astype(F32)
    third = rest - second
    return first + pltpu.roll(second, 32, 1) + pltpu.roll(third, 64, 1)


def from_pieces(packed):
    back = LANES
    return packed + pltpu.roll(packed, back - 32, 1) + pltpu.roll(packed, back - 64, 1)


def columns_kernel(field_ref, table_ref, out_ref, total):
    chans, rows, tile = field_ref.shape
    lanes = table_ref.shape[1]
    step = pl.program_id(0)
    part = dot(field_ref[...].reshape(chans * rows, tile), table_ref[...])

    @pl.when(step == 0)
    def _():
        total[...] = part

    @pl.when(step > 0)
    def _():
        total[...] += part

    @pl.when(step == pl.num_programs(0) - 1)
    def _():
        for c in range(chans):
            out_ref[:, c * lanes : (c + 1) * lanes] = total[c * rows : (c + 1) * rows].astype(BF16)


def rows_kernel(chans, modes, scale, extra, mine_ref, other_ref, phase_ref, *outs):
    half = phase_ref.shape[0] // 2
    lanes = 2 * modes
    phase = phase_ref[...]
    for c in range(chans):
        at = slice(c * lanes, (c + 1) * lanes)
        both = jnp.concatenate([mine_ref[:, at], other_ref[:, at]], axis=0)
        part = dot(phase, both)
        real = part[:half, :modes] + part[half:, modes:]
        imag = part[:half, modes:] - part[half:, :modes]
        full = (scale * jnp.concatenate([real, imag], axis=1)).astype(BF16)
        size = half // len(outs)
        for d, out in enumerate(outs):
            out[:, at] = full[d * size : (d + 1) * size]
    if extra:
        top = chans * lanes
        rows = chans
        total = from_pieces(mine_ref[:rows, top:].astype(F32)) + from_pieces(
            other_ref[:rows, top:].astype(F32)
        )
        packed = to_pieces(keep_low(total)).astype(BF16)
        for out in outs:
            put_pieces(out, packed, top, rows)


def keep_low(value):
    lane = lax.broadcasted_iota(jnp.int32, value.shape, 1)
    return jnp.where(lane < 32, value, 0.0)


def put_pieces(out, packed, top, rows):
    size = out.shape[0]
    if size >= rows:
        out[:rows, top : top + LANES] = packed
        if size > rows:
            out[rows:, top : top + LANES] = jnp.zeros((size - rows, LANES), packed.dtype)
        return
    for e in range(rows // size):
        out[:, top + e * LANES : top + (e + 1) * LANES] = packed[e * size : (e + 1) * size]


def get_pieces(ref, top, rows):
    size = ref.shape[0]
    if size >= rows:
        return ref[:rows, top : top + LANES].astype(F32)
    return jnp.concatenate(
        [
            ref[:, top + e * LANES : top + (e + 1) * LANES].astype(F32)
            for e in range(rows // size)
        ],
        axis=0,
    )


def mix_kernel(chans, modes, count, weight_ref, *refs):
    chunks = refs[:count]
    mixed_ref, spectrum_ref, sums = refs[count:]
    lanes = 2 * modes
    for c in range(2 * chans):
        at = slice(c * modes, (c + 1) * modes)
        value = tree([chunk[:, at].astype(F32) for chunk in chunks])
        sums[c] = value
        spectrum_ref[:, at] = value.astype(BF16)

    for o in range(chans):
        real = imag = None
        for c in range(chans):
            wr = weight_ref[0, c, o].astype(F32)
            wi = weight_ref[1, c, o].astype(F32)
            fr = sums[2 * c]
            fi = sums[2 * c + 1]
            a = wr * fr - wi * fi
            b = wr * fi + wi * fr
            real = a if real is None else real + a
            imag = b if imag is None else imag + b
        mixed_ref[:, o * lanes : o * lanes + modes] = real.astype(BF16)
        mixed_ref[:, o * lanes + modes : (o + 1) * lanes] = imag.astype(BF16)


def back_kernel(chans, modes, count, maps, where_ref, weight_ref, *refs):
    chunks = refs[:count]
    back_ref = refs[count]
    slices = refs[count + 1 : count + 1 + maps]
    sums, gathered = refs[count + 1 + maps :]
    lanes = 2 * modes
    shape = (chunks[0].shape[0], modes)
    doubling = jnp.where(lax.broadcasted_iota(jnp.int32, shape, 1) == 0, 1.0, 2.0)
    for c in range(2 * chans):
        at = slice(c * modes, (c + 1) * modes)
        value = tree([chunk[:, at].astype(F32) for chunk in chunks]) * doubling
        sums[c] = value
        gathered[:, at] = value.astype(BF16)

    for c in range(chans):
        real = imag = None
        for o in range(chans):
            wr = weight_ref[0, c, o].astype(F32)
            wi = weight_ref[1, c, o].astype(F32)
            gr = sums[2 * o]
            gi = sums[2 * o + 1]
            a = wr * gr + wi * gi
            b = wr * gi - wi * gr
            real = a if real is None else real + a
            imag = b if imag is None else imag + b
        back_ref[:, c * lanes : c * lanes + modes] = real.astype(BF16)
        back_ref[:, c * lanes + modes : (c + 1) * lanes] = imag.astype(BF16)

    top = chans * lanes
    total = tree([from_pieces(get_pieces(chunk, top, chans)) for chunk in chunks])
    packed = to_pieces(keep_low(total)).astype(BF16)
    span = chans // maps * lanes
    for d, out in enumerate(slices):
        first = pl.multiple_of((where_ref[0] ^ d) * span, LANES)
        out[:, :span] = gathered[:, pl.ds(first, span)]
        put_pieces(out, packed, span, chans)


def weight_kernel(chans, modes, maps, scale, *refs):
    spectra = refs[:maps]
    slices = refs[maps : 2 * maps]
    grad_ref, local_ref, bias_ref = refs[2 * maps :]
    lanes = 2 * modes
    part = chans // maps
    for o in range(part):
        at = o * lanes
        grads = [
            (s[:, at : at + modes].astype(F32), s[:, at + modes : at + lanes].astype(F32))
            for s in slices
        ]
        for c in range(grad_ref.shape[1]):
            at = c * lanes
            real = []
            imag = []
            for spectrum, (gr, gi) in zip(spectra, grads):
                fr = spectrum[:, at : at + modes].astype(F32)
                fi = spectrum[:, at + modes : at + lanes].astype(F32)
                real.append(gr * fr + gi * fi)
                imag.append(gi * fr - gr * fi)
            grad_ref[0, c, o] = tree(real)
            grad_ref[1, c, o] = tree(imag)

    @pl.when(pl.program_id(0) == 0)
    def _():
        small = [from_pieces(get_pieces(s, part * lanes, chans)) for s in slices]
        small = scale * tree(small)
        local_ref[...] = small[:, :chans]
        bias_ref[...] = pltpu.roll(small, LANES - chans, 1)[:1, :chans]


def channel_map(local_ref, chans, back):
    size = chans * GROUP
    pick = (
        lax.broadcasted_iota(jnp.int32, (size, chans), 0) // GROUP
        == lax.broadcasted_iota(jnp.int32, (size, chans), 1)
    )
    pick = jnp.where(pick, 1.0, 0.0).astype(BF16)
    local = local_ref[...]
    if back:
        wide = dot(pick, local).astype(BF16)
    else:
        wide = lax.dot_general(
            pick, local, (((1,), (1,)), ((), ())), preferred_element_type=F32
        ).astype(BF16)
    full = dot_nt(wide, pick)
    row = lax.broadcasted_iota(jnp.int32, (size, size), 0) % GROUP
    lane = lax.broadcasted_iota(jnp.int32, (size, size), 1) % GROUP
    return jnp.where(row == lane, full, 0.0).astype(BF16)


def inverse_rows(chans, modes, scale, phase, chunks, doubled, out):
    lanes = 2 * modes
    half = phase.shape[0] // 2
    factor = jnp.full((1, modes), scale, F32)
    if doubled:
        first = lax.broadcasted_iota(jnp.int32, (1, modes), 1) == 0
        factor = jnp.where(first, scale, 2.0 * scale)
    for o in range(chans):
        at = slice(o * lanes, (o + 1) * lanes)
        part = dot(phase, jnp.concatenate([chunk[:, at] for chunk in chunks], axis=0))
        real = (part[:half, :modes] - part[half:, modes:]) * factor
        imag = (part[:half, modes:] + part[half:, :modes]) * factor
        out[o * half : (o + 1) * half, :modes] = real.astype(BF16)
        out[o * half : (o + 1) * half, modes:] = imag.astype(BF16)


SLOPE = math.sqrt(2.0 / math.pi)
CUBIC = 0.044715


def gelu_slope(x):
    kind = x.dtype.type
    square = x * x
    inner = x * (kind(SLOPE) + kind(SLOPE * CUBIC) * square)
    outer = x * (kind(0.5 * SLOPE) + kind(1.5 * SLOPE * CUBIC) * square)
    t = jnp.tanh(inner)
    return (kind(1.0) + t) * (kind(0.5) + (kind(1.0) - t) * outer)


def main_kernel(chans, modes, scale, count, *refs):
    chunks = refs[:count]
    (phase_ref, inverse_ref, forward_ref, local_ref, bias_ref, field_ref, cot_ref) = refs[
        count : count + 7
    ]
    grad_ref, sums_ref, rows, mixer, wide, total, outer = refs[count + 7 :]
    step = pl.program_id(0)
    size = chans * GROUP
    here, tile = field_ref.shape[1:]
    lanes = 2 * modes

    @pl.when(step == 0)
    def _():
        inverse_rows(chans, modes, scale, phase_ref[...], chunks, True, rows)
        mixer[...] = channel_map(local_ref, chans, False)
        total[...] = jnp.zeros_like(total)
        outer[...] = jnp.zeros_like(outer)
        sums_ref[...] = jnp.zeros_like(sums_ref)

    mix = mixer[...]
    group = lax.broadcasted_iota(jnp.int32, (size, chans), 0) // GROUP
    pick = group == lax.broadcasted_iota(jnp.int32, (size, chans), 1)
    bias = jnp.sum(jnp.where(pick, bias_ref[...], 0.0), axis=1, keepdims=True)
    wide[...] = dot(rows[...], inverse_ref[...]).reshape(chans, here, tile)
    both = jnp.zeros((size, size), F32)
    for at in range(0, here, GROUP):
        block = slice(at, at + GROUP)
        field = field_ref[:, block, :].reshape(size, tile)
        preact = dot(mix, field) + wide[:, block, :].reshape(size, tile) + bias
        cot = cot_ref[:, block, :].reshape(size, tile)
        grad = cot * gelu_slope(preact.astype(BF16))
        grad_ref[:, block, :] = grad.reshape(chans, GROUP, tile)
        both = both + dot_nt(field, grad)
    outer[...] += both
    total[...] += dot(grad_ref[...].reshape(chans * here, tile), forward_ref[...])

    @pl.when(step == pl.num_programs(0) - 1)
    def _():
        for o in range(chans):
            sums_ref[:, o * lanes : (o + 1) * lanes] = total[o * here : (o + 1) * here].astype(BF16)
        row = lax.broadcasted_iota(jnp.int32, (size, size), 0) % GROUP
        lane = lax.broadcasted_iota(jnp.int32, (size, size), 1) % GROUP
        same = jnp.where(row == lane, outer[...], 0.0).reshape(chans, GROUP, size)
        folded = jnp.sum(same, axis=1)
        wider = lax.broadcasted_iota(jnp.int32, (size, LANES), 0) // GROUP
        gather = wider == lax.broadcasted_iota(jnp.int32, (size, LANES), 1)
        local = jnp.dot(
            folded,
            jnp.where(gather, 1.0, 0.0),
            precision=lax.Precision.HIGHEST,
            preferred_element_type=F32,
        )
        biases = jnp.sum(total[:, :modes].reshape(chans, here, modes), axis=1)[:, :1]
        place = lax.broadcasted_iota(jnp.int32, (chans, LANES), 1)
        line = lax.broadcasted_iota(jnp.int32, (chans, LANES), 0)
        across = jnp.sum(jnp.where(place == chans + line, biases, 0.0), axis=0, keepdims=True)
        small = jnp.where(place < chans, local, jnp.where(line == 0, across, 0.0))
        sums_ref[:chans, chans * lanes :] = to_pieces(small).astype(BF16)


def field_kernel(chans, modes, scale, count, *refs):
    chunks = refs[:count]
    phase_ref, inverse_ref, local_ref, grad_ref, out_ref, rows, mixer, wide = refs[count:]
    size = chans * GROUP
    here, tile = grad_ref.shape[1:]

    @pl.when(pl.program_id(0) == 0)
    def _():
        inverse_rows(chans, modes, scale, phase_ref[...], chunks, False, rows)
        mixer[...] = channel_map(local_ref, chans, True)

    mix = mixer[...]
    wide[...] = dot(rows[...], inverse_ref[...]).reshape(chans, here, tile)
    for at in range(0, here, GROUP):
        block = slice(at, at + GROUP)
        value = dot(mix, grad_ref[:, block, :].reshape(size, tile))
        value = value + wide[:, block, :].reshape(size, tile)
        out_ref[:, block, :] = value.astype(BF16).reshape(chans, GROUP, tile)


def swap(value, axis, mask):
    size = lax.axis_size(axis)
    return lax.ppermute(value, axis, [(at, at ^ mask) for at in range(size)])


def on_device(fields, cotangent, spectral, local_weight, bias):
    field = fields[0]
    cot = cotangent[0]
    chans, rows_here, width = field.shape
    owned, modes = spectral.shape[3:]
    row_count = lax.axis_size("row")
    map_count = lax.axis_size("dp")
    chips = row_count // 2
    height = rows_here * row_count
    scale = 1.0 / math.sqrt(height * width)
    grad_scale = 1.0 / math.sqrt(map_count * height * width)
    lanes = 2 * modes
    flat = chans * lanes
    size = chans * GROUP
    extra = LANES * max(1, chans // owned)
    assert 2 * chans <= 32
    aligned = owned % GROUP == 0

    me = lax.axis_index("row")
    chip, core = me // 2, me % 2
    inverse_const = column_table(width, modes)
    inverse = jnp.asarray(inverse_const)
    forward = jnp.asarray(np.ascontiguousarray(inverse_const.T))

    near = jnp.arange(chips, dtype=jnp.int32) ^ chip
    inner = jnp.arange(owned, dtype=jnp.int32)
    own_modes = ((2 * near + core)[:, None] * owned + inner[None, :]).reshape(-1)
    far_modes = ((2 * near + 1 - core)[:, None] * owned + inner[None, :]).reshape(-1)
    here = jnp.arange(rows_here, dtype=jnp.int32)
    pair_rows = jnp.concatenate([me * rows_here + here, (me ^ 1) * rows_here + here])
    angle = row_angles(own_modes, pair_rows, height, modes)
    to_modes = jnp.concatenate([jnp.cos(angle), jnp.sin(angle)], axis=0).astype(BF16)
    all_modes = jnp.concatenate([own_modes, far_modes])
    angle = row_angles(all_modes, me * rows_here + here, height, modes).T
    to_rows = jnp.concatenate([jnp.cos(angle), jnp.sin(angle)], axis=0).astype(BF16)

    tile = min(TILE, width)
    tiles = width // tile
    block = pl.BlockSpec((chans, rows_here, tile), lambda i: (0, 0, i))
    inverse_block = pl.BlockSpec((lanes, tile), lambda i: (0, i))
    forward_block = pl.BlockSpec((tile, lanes), lambda i: (i, 0))

    def rows_step(mine, other, more):
        out_lanes = flat + (extra if more else 0)
        if aligned:
            shapes = [jax.ShapeDtypeStruct((owned, out_lanes), BF16)] * chips
        else:
            shapes = [jax.ShapeDtypeStruct((chips * owned, flat), BF16)]
        kernel = functools.partial(rows_kernel, chans, modes, scale, more and aligned)
        outs = pl.pallas_call(
            kernel,
            name="rows",
            out_shape=shapes,
            compiler_params=room(8),
            cost_estimate=pl.CostEstimate(
                flops=4 * chips * owned * 2 * rows_here * flat,
                transcendentals=0,
                bytes_accessed=6 * rows_here * flat,
            ),
        )(mine, other, to_modes)
        if aligned:
            return outs
        pieces = jnp.split(outs[0], chips, axis=0)
        if more:
            packed = small_sum(mine[:chans, flat:], other[:chans, flat:])
            packed = packed.reshape(chans // owned, owned, LANES).transpose(1, 0, 2)
            packed = packed.reshape(owned, extra)
            pieces = [jnp.concatenate([piece, packed], axis=1) for piece in pieces]
        return pieces

    def small_sum(mine, other):
        def kernel(a, b, out):
            total = from_pieces(a[...].astype(F32)) + from_pieces(b[...].astype(F32))
            out[...] = to_pieces(keep_low(total)).astype(BF16)

        return pl.pallas_call(
            kernel, name="small", out_shape=jax.ShapeDtypeStruct((chans, LANES), BF16)
        )(mine, other)

    def spread(pieces):
        return [pieces[0]] + [swap(pieces[d], "row", 2 * d) for d in range(1, chips)]

    def gather(piece):
        same = [piece] + [swap(piece, "row", 2 * d) for d in range(1, chips)]
        chunks = same + [swap(part, "row", 1) for part in same]
        return chunks if aligned else [jnp.concatenate(chunks, axis=0)]

    coeffs = pl.pallas_call(
        columns_kernel,
        name="columns",
        grid=(tiles,),
        in_specs=[block, forward_block],
        out_specs=whole((rows_here, flat)),
        out_shape=jax.ShapeDtypeStruct((rows_here, flat), BF16),
        scratch_shapes=[pltpu.VMEM((chans * rows_here, lanes), F32)],
        compiler_params=room(12),
    )(streamed(field), streamed(forward))
    chunks = spread(rows_step(coeffs, swap(coeffs, "row", 1), False))

    mixed, spectrum = pl.pallas_call(
        functools.partial(mix_kernel, chans, modes, chips),
        name="mix",
        out_shape=[jax.ShapeDtypeStruct((owned, flat), BF16)] * 2,
        scratch_shapes=[pltpu.VMEM((2 * chans, owned, modes), F32)],
        compiler_params=room(10),
    )(spectral, *chunks)
    mixed = gather(mixed)
    spectra = [spectrum] + [swap(spectrum, "dp", d) for d in range(1, map_count)]

    chunk_specs = [whole(part.shape) for part in mixed]
    main = pl.pallas_call(
        functools.partial(main_kernel, chans, modes, scale, len(mixed)),
        name="main",
        grid=(tiles,),
        in_specs=chunk_specs
        + [
            whole(to_rows.shape),
            inverse_block,
            forward_block,
            whole((chans, chans)),
            whole((1, chans)),
            block,
            block,
        ],
        out_specs=[block, whole((rows_here, flat + LANES))],
        out_shape=[
            pltpu.HBM(field.shape, BF16),
            jax.ShapeDtypeStruct((rows_here, flat + LANES), BF16),
        ],
        scratch_shapes=[
            pltpu.VMEM((chans * rows_here, lanes), BF16),
            pltpu.VMEM((size, size), BF16),
            pltpu.VMEM((chans, rows_here, tile), F32),
            pltpu.VMEM((chans * rows_here, lanes), F32),
            pltpu.VMEM((size, size), F32),
        ],
        compiler_params=room(28),
    )
    grad_pre, grad_coeffs = main(
        *mixed, to_rows, streamed(inverse), streamed(forward), local_weight, bias[None], streamed(field), streamed(cot)
    )

    chunks = spread(rows_step(grad_coeffs, swap(grad_coeffs, "row", 1), True))
    part_lanes = chans // map_count * lanes
    outs = pl.pallas_call(
        functools.partial(back_kernel, chans, modes, chips, map_count),
        name="back",
        in_specs=[pl.BlockSpec(memory_space=pltpu.SMEM)]
        + [pl.BlockSpec(memory_space=pltpu.VMEM)] * (1 + chips),
        out_shape=[jax.ShapeDtypeStruct((owned, flat), BF16)]
        + [jax.ShapeDtypeStruct((owned, part_lanes + extra), BF16)] * map_count,
        scratch_shapes=[
            pltpu.VMEM((2 * chans, owned, modes), F32),
            pltpu.VMEM((owned, flat), BF16),
        ],
        compiler_params=room(10),
    )(lax.axis_index("dp").astype(jnp.int32)[None], spectral, *chunks)
    freq_grad = gather(outs[0])
    slices = [outs[1]] + [swap(outs[1 + d], "dp", d) for d in range(1, map_count)]

    steps = 4 if chans % 4 == 0 else 1
    spectral_grad, local_grad, bias_grad = pl.pallas_call(
        functools.partial(weight_kernel, chans, modes, map_count, grad_scale),
        name="weights",
        grid=(steps,),
        in_specs=[pl.BlockSpec((owned, flat // steps), lambda i: (0, i))] * map_count
        + [whole(slices[0].shape)] * map_count,
        out_specs=[
            pl.BlockSpec(
                (2, chans // steps, chans // map_count, owned, modes), lambda i: (0, i, 0, 0, 0)
            ),
            whole((chans, chans)),
            whole((1, chans)),
        ],
        out_shape=[
            pltpu.HBM((2, chans, chans // map_count, owned, modes), F32),
            jax.ShapeDtypeStruct((chans, chans), F32),
            jax.ShapeDtypeStruct((1, chans), F32),
        ],
        compiler_params=room(12),
    )(*spectra, *slices)

    final = pl.pallas_call(
        functools.partial(field_kernel, chans, modes, scale, len(freq_grad)),
        name="field",
        grid=(tiles,),
        in_specs=[whole(part.shape) for part in freq_grad]
        + [whole(to_rows.shape), inverse_block, whole((chans, chans)), block],
        out_specs=block,
        out_shape=pltpu.HBM(field.shape, BF16),
        scratch_shapes=[
            pltpu.VMEM((chans * rows_here, lanes), BF16),
            pltpu.VMEM((size, size), BF16),
            pltpu.VMEM((chans, rows_here, tile), F32),
        ],
        compiler_params=room(20),
    )
    field_grad = final(
        *freq_grad, to_rows, streamed(inverse), local_weight, streamed(grad_pre)
    )

    return (field_grad[None], spectral_grad, local_grad, bias_grad[0])


def solution(mesh):
    return jax.shard_map(
        on_device,
        mesh=mesh,
        in_specs=(
            P("dp", None, "row", None),
            P("dp", None, "row", None),
            P(None, None, None, "row", None),
            P(),
            P(),
        ),
        out_specs=(P("dp", None, "row", None), P(None, None, "dp", "row", None), P(), P()),
        check_vma=False,
    )
```

profile of v0, /device:TPU:0, one launch (start us, length us, event | category | flops | bytes accessed | tf_op | source)
XLA Modules:
  0.0 89.2 jit_solution(1592568595443380836)
XLA Ops:
  0.7 4.5 %columns.1.mine_ref = bf16[64,4096]{1,0:T(8,128)(2,1)S(1)} custom-call(bf16[16,64,2048]{2,1,0:T(8,128)(2,1)} %bitcast.7, bf16[2048,256]{1,0:T(8,128)(2,1)} %constant.90.clone.table_ref.refs_10_), custom_call_target="tpu_custom_call" | custom-call | tf_op jit(solution)/shard_map/columns/pallas_call | solution.py:463
  5.1 0.6 collective-permute-start
  5.7 0.1 iota_add_fusion.1
  5.8 0.1 add.131
  5.9 0.1 pad_add_fusion
  5.9 0.2 cosine_convert_fusion.1
  6.2 1.0 %collective-permute-done.other_ref = bf16[64,4096]{1,0:T(8,128)(2,1)S(1)} collective-permute-done((bf16[64,4096]{1,0:T(8,128)(2,1)S(1)}, bf16[64,4096]{1,0:T(8,128)(2,1)S(1)}, u32[]{:S(2)}, u32[]{:S(2)}) %collective-permute-start) | collective-permute-done | bytes 524320 | tf_op jit(solution)/shard_map/ppermute | solution.py:373
  7.2 0.4 rows.2
  7.7 2.9 %collective-permute-start.1 = (bf16[16,4096]{1,0:T(8,128)(2,1)S(1)}, bf16[16,4096]{1,0:T(8,128)(2,1)S(1)}, u32[]{:S(2)}, u32[]{:S(2)}) collective-permute-start(bf16[16,4096]{1,0:T(8,128)(2,1)S(1)} %get-tuple-element.25), channel_id=1, source_target_pairs={{0,2},{1,3},{2,0},{3,1},{4,6},{5,7},{6,4},{7,5},{8,10},{9,11},{10,... | collective-permute-start | bytes 393224 | tf_op jit(solution)/shard_map/ppermute | solution.py:373
  10.6 1.5 %collective-permute-start.2 = (bf16[16,4096]{1,0:T(8,128)(2,1)S(1)}, bf16[16,4096]{1,0:T(8,128)(2,1)S(1)}, u32[]{:S(2)}, u32[]{:S(2)}) collective-permute-start(bf16[16,4096]{1,0:T(8,128)(2,1)S(1)} %get-tuple-element.26), channel_id=1, source_target_pairs={{0,4},{1,5},{2,6},{3,7},{4,0},{5,1},{6,2},{7,3},{8,12},{9,13},{10,... | collective-permute-start | bytes 393224 | tf_op jit(solution)/shard_map/ppermute | solution.py:373
  12.1 0.0 collective-permute-start.3
  12.1 2.4 %collective-permute-done.1.refs_1_ = bf16[16,4096]{1,0:T(8,128)(2,1)S(1)} collective-permute-done((bf16[16,4096]{1,0:T(8,128)(2,1)S(1)}, bf16[16,4096]{1,0:T(8,128)(2,1)S(1)}, u32[]{:S(2)}, u32[]{:S(2)}) %collective-permute-start.1) | collective-permute-done | bytes 131104 | tf_op jit(solution)/shard_map/ppermute | solution.py:373
  14.5 4.1 %collective-permute-done.2.refs_2_ = bf16[16,4096]{1,0:T(8,128)(2,1)S(1)} collective-permute-done((bf16[16,4096]{1,0:T(8,128)(2,1)S(1)}, bf16[16,4096]{1,0:T(8,128)(2,1)S(1)}, u32[]{:S(2)}, u32[]{:S(2)}) %collective-permute-start.2) | collective-permute-done | bytes 131104 | tf_op jit(solution)/shard_map/ppermute | solution.py:373
  18.6 0.0 collective-permute-done.3.refs_3_
  18.6 0.7 mix.1
  19.4 1.3 %collective-permute-start.4 = (bf16[16,4096]{1,0:T(8,128)(2,1)S(1)}, bf16[16,4096]{1,0:T(8,128)(2,1)S(1)}, u32[]{:S(2)}, u32[]{:S(2)}) collective-permute-start(bf16[16,4096]{1,0:T(8,128)(2,1)S(1)} %get-tuple-element.28.refs_0_), channel_id=1, source_target_pairs={{0,2},{1,3},{2,0},{3,1},{4,6},{5,7},{6,4},{7,5},{8,10},{9,11},{10,... | collective-permute-start | bytes 393224 | tf_op jit(solution)/shard_map/ppermute | solution.py:373
  20.7 0.8 collective-permute-start.5
  21.5 1.4 %collective-permute-start.6 = (bf16[16,4096]{1,0:T(8,128)(2,1)S(1)}, bf16[16,4096]{1,0:T(8,128)(2,1)S(1)}, u32[]{:S(2)}, u32[]{:S(2)}) collective-permute-start(bf16[16,4096]{1,0:T(8,128)(2,1)S(1)} %get-tuple-element.28.refs_0_), channel_id=1, source_target_pairs={{0,6},{1,7},{2,4},{3,5},{4,2},{5,3},{6,0},{7,1},{8,14},{9,15},{10,... | collective-permute-start | bytes 393224 | tf_op jit(solution)/shard_map/ppermute | solution.py:373
  22.9 0.1 iota_add_fusion
  23.0 0.1 add.142
  23.1 0.1 and_select_fusion
  23.2 0.0 collective-permute-start.7
  23.2 2.2 %collective-permute-done.4.refs_1_ = bf16[16,4096]{1,0:T(8,128)(2,1)S(1)} collective-permute-done((bf16[16,4096]{1,0:T(8,128)(2,1)S(1)}, bf16[16,4096]{1,0:T(8,128)(2,1)S(1)}, u32[]{:S(2)}, u32[]{:S(2)}) %collective-permute-start.4) | collective-permute-done | bytes 131104 | tf_op jit(solution)/shard_map/ppermute | solution.py:373
  25.4 0.0 collective-permute-start.8
  25.4 2.6 %collective-permute-done.5.refs_2_ = bf16[16,4096]{1,0:T(8,128)(2,1)S(1)} collective-permute-done((bf16[16,4096]{1,0:T(8,128)(2,1)S(1)}, bf16[16,4096]{1,0:T(8,128)(2,1)S(1)}, u32[]{:S(2)}, u32[]{:S(2)}) %collective-permute-start.5) | collective-permute-done | bytes 131104 | tf_op jit(solution)/shard_map/ppermute | solution.py:373
  27.9 0.0 collective-permute-start.9
  27.9 0.0 collective-permute-done.6.refs_3_
  27.9 0.5 collective-permute-start.10
  28.4 0.2 cosine_convert_fusion
  28.7 0.0 collective-permute-done.7.refs_4_
  28.7 0.0 collective-permute-done.8.refs_5_
  28.7 0.6 collective-permute-done.9.refs_6_
  29.3 0.2 collective-permute-done.10.refs_7_
  29.5 12.6 %main.1 = (bf16[16,64,2048]{2,1,0:T(8,128)(2,1)}, bf16[64,4224]{1,0:T(8,128)(2,1)S(1)}) custom-call(bf16[16,4096]{1,0:T(8,128)(2,1)S(1)} %get-tuple-element.28.refs_0_, bf16[16,4096]{1,0:T(8,128)(2,1)S(1)} %collective-permute-done.4.refs_1_, bf16[16,4096]{1,0:T(8,128)(2,1)S(1)} %collective-permute-done.5.refs_2_, ...), custom_call_target="tpu_custom_call" | custom-call | tf_op jit(solution)/shard_map/main/pallas_call | solution.py:514
  42.0 0.3 collective-permute-start.11
  42.4 1.6 %collective-permute-done.11.other_ref = bf16[64,4224]{1,0:T(8,128)(2,1)S(1)} collective-permute-done((bf16[64,4224]{1,0:T(8,128)(2,1)S(1)}, bf16[64,4224]{1,0:T(8,128)(2,1)S(1)}, u32[]{:S(2)}, u32[]{:S(2)}) %collective-permute-start.11) | collective-permute-done | bytes 540704 | tf_op jit(solution)/shard_map/ppermute | solution.py:373
  44.0 0.4 rows.3
  44.4 1.4 %collective-permute-start.12 = (bf16[16,4224]{1,0:T(8,128)(2,1)S(1)}, bf16[16,4224]{1,0:T(8,128)(2,1)S(1)}, u32[]{:S(2)}, u32[]{:S(2)}) collective-permute-start(bf16[16,4224]{1,0:T(8,128)(2,1)S(1)} %get-tuple-element.31), channel_id=1, source_target_pairs={{0,2},{1,3},{2,0},{3,1},{4,6},{5,7},{6,4},{7,5},{8,10},{9,11},{10,... | collective-permute-start | bytes 405512 | tf_op jit(solution)/shard_map/ppermute | solution.py:373
  45.8 0.9 collective-permute-start.13
  46.6 1.3 %collective-permute-start.14 = (bf16[16,4224]{1,0:T(8,128)(2,1)S(1)}, bf16[16,4224]{1,0:T(8,128)(2,1)S(1)}, u32[]{:S(2)}, u32[]{:S(2)}) collective-permute-start(bf16[16,4224]{1,0:T(8,128)(2,1)S(1)} %get-tuple-element.33), channel_id=1, source_target_pairs={{0,6},{1,7},{2,4},{3,5},{4,2},{5,3},{6,0},{7,1},{8,14},{9,15},{10,... | collective-permute-start | bytes 405512 | tf_op jit(solution)/shard_map/ppermute | solution.py:373
  47.9 1.6 %collective-permute-start.22 = (bf16[16,4096]{1,0:T(8,128)(2,1)S(1)}, bf16[16,4096]{1,0:T(8,128)(2,1)S(1)}, u32[]{:S(2)}, u32[]{:S(2)}) collective-permute-start(bf16[16,4096]{1,0:T(8,128)(2,1)S(1)} %get-tuple-element.36.refs_0_), channel_id=1, source_target_pairs={{0,8},{8,0},{16,24},{24,16},{1,9},{9,1},{17,25},{25,17},{2,10},{10... | collective-permute-start | bytes 393224 | tf_op jit(solution)/shard_map/ppermute | solution.py:373
  49.5 2.6 %collective-permute-start.23 = (bf16[16,4096]{1,0:T(8,128)(2,1)S(1)}, bf16[16,4096]{1,0:T(8,128)(2,1)S(1)}, u32[]{:S(2)}, u32[]{:S(2)}) collective-permute-start(bf16[16,4096]{1,0:T(8,128)(2,1)S(1)} %get-tuple-element.36.refs_0_), channel_id=1, source_target_pairs={{0,16},{8,24},{16,0},{24,8},{1,17},{9,25},{17,1},{25,9},{2,18},{10... | collective-permute-start | bytes 393224 | tf_op jit(solution)/shard_map/ppermute | solution.py:373
  52.1 0.0 collective-permute-done.12.refs_1_
  52.1 2.1 %collective-permute-done.13.refs_2_ = bf16[16,4224]{1,0:T(8,128)(2,1)S(1)} collective-permute-done((bf16[16,4224]{1,0:T(8,128)(2,1)S(1)}, bf16[16,4224]{1,0:T(8,128)(2,1)S(1)}, u32[]{:S(2)}, u32[]{:S(2)}) %collective-permute-start.13) | collective-permute-done | bytes 135200 | tf_op jit(solution)/shard_map/ppermute | solution.py:373
  54.2 0.8 back.1
  55.0 0.8 collective-permute-start.15
  55.8 1.3 %collective-permute-start.16 = (bf16[16,4096]{1,0:T(8,128)(2,1)S(1)}, bf16[16,4096]{1,0:T(8,128)(2,1)S(1)}, u32[]{:S(2)}, u32[]{:S(2)}) collective-permute-start(bf16[16,4096]{1,0:T(8,128)(2,1)S(1)} %get-tuple-element.34.refs_0_), channel_id=1, source_target_pairs={{0,4},{1,5},{2,6},{3,7},{4,0},{5,1},{6,2},{7,3},{8,12},{9,13},{10,... | collective-permute-start | bytes 393224 | tf_op jit(solution)/shard_map/ppermute | solution.py:373
  57.1 1.5 %collective-permute-start.17 = (bf16[16,4096]{1,0:T(8,128)(2,1)S(1)}, bf16[16,4096]{1,0:T(8,128)(2,1)S(1)}, u32[]{:S(2)}, u32[]{:S(2)}) collective-permute-start(bf16[16,4096]{1,0:T(8,128)(2,1)S(1)} %get-tuple-element.34.refs_0_), channel_id=1, source_target_pairs={{0,6},{1,7},{2,4},{3,5},{4,2},{5,3},{6,0},{7,1},{8,14},{9,15},{10,... | collective-permute-start | bytes 393224 | tf_op jit(solution)/shard_map/ppermute | solution.py:373
  58.6 3.6 %collective-permute-start.24 = (bf16[16,4096]{1,0:T(8,128)(2,1)S(1)}, bf16[16,4096]{1,0:T(8,128)(2,1)S(1)}, u32[]{:S(2)}, u32[]{:S(2)}) collective-permute-start(bf16[16,4096]{1,0:T(8,128)(2,1)S(1)} %get-tuple-element.36.refs_0_), channel_id=1, source_target_pairs={{0,24},{8,16},{16,8},{24,0},{1,25},{9,17},{17,9},{25,1},{2,26},{10... | collective-permute-start | bytes 393224 | tf_op jit(solution)/shard_map/ppermute | solution.py:373
  62.2 0.0 collective-permute-done.15.refs_1_
  62.2 0.5 collective-permute-start.19
  62.7 0.9 collective-permute-done.16.refs_2_
  63.6 0.0 collective-permute-start.20
  63.6 0.5 collective-permute-start.21
  64.1 1.4 %collective-permute-done.24.refs_3_ = bf16[16,4096]{1,0:T(8,128)(2,1)S(1)} collective-permute-done((bf16[16,4096]{1,0:T(8,128)(2,1)S(1)}, bf16[16,4096]{1,0:T(8,128)(2,1)S(1)}, u32[]{:S(2)}, u32[]{:S(2)}) %collective-permute-start.24) | collective-permute-done | bytes 131104 | tf_op jit(solution)/shard_map/ppermute | solution.py:373
  65.5 1.3 %collective-permute-start.25 = (bf16[16,1152]{1,0:T(8,128)(2,1)S(1)}, bf16[16,1152]{1,0:T(8,128)(2,1)S(1)}, u32[]{:S(2)}, u32[]{:S(2)}) collective-permute-start(bf16[16,1152]{1,0:T(8,128)(2,1)S(1)} %get-tuple-element.38), channel_id=1, source_target_pairs={{0,8},{8,0},{16,24},{24,16},{1,9},{9,1},{17,25},{25,17},{2,10},{10... | collective-permute-start | bytes 110600 | tf_op jit(solution)/shard_map/ppermute | solution.py:373
  66.8 2.7 %collective-permute-done.25.refs_5_ = bf16[16,1152]{1,0:T(8,128)(2,1)S(1)} collective-permute-done((bf16[16,1152]{1,0:T(8,128)(2,1)S(1)}, bf16[16,1152]{1,0:T(8,128)(2,1)S(1)}, u32[]{:S(2)}, u32[]{:S(2)}) %collective-permute-start.25) | collective-permute-done | bytes 36896 | tf_op jit(solution)/shard_map/ppermute | solution.py:373
  69.4 3.1 %collective-permute-start.26 = (bf16[16,1152]{1,0:T(8,128)(2,1)S(1)}, bf16[16,1152]{1,0:T(8,128)(2,1)S(1)}, u32[]{:S(2)}, u32[]{:S(2)}) collective-permute-start(bf16[16,1152]{1,0:T(8,128)(2,1)S(1)} %get-tuple-element.39), channel_id=1, source_target_pairs={{0,16},{8,24},{16,0},{24,8},{1,17},{9,25},{17,1},{25,9},{2,18},{10... | collective-permute-start | bytes 110600 | tf_op jit(solution)/shard_map/ppermute | solution.py:373
  72.5 1.9 %collective-permute-done.26.refs_6_ = bf16[16,1152]{1,0:T(8,128)(2,1)S(1)} collective-permute-done((bf16[16,1152]{1,0:T(8,128)(2,1)S(1)}, bf16[16,1152]{1,0:T(8,128)(2,1)S(1)}, u32[]{:S(2)}, u32[]{:S(2)}) %collective-permute-start.26) | collective-permute-done | bytes 36896 | tf_op jit(solution)/shard_map/ppermute | solution.py:373
  74.4 3.4 %collective-permute-start.27 = (bf16[16,1152]{1,0:T(8,128)(2,1)S(1)}, bf16[16,1152]{1,0:T(8,128)(2,1)S(1)}, u32[]{:S(2)}, u32[]{:S(2)}) collective-permute-start(bf16[16,1152]{1,0:T(8,128)(2,1)S(1)} %get-tuple-element.40), channel_id=1, source_target_pairs={{0,24},{8,16},{16,8},{24,0},{1,25},{9,17},{17,9},{25,1},{2,26},{10... | collective-permute-start | bytes 110600 | tf_op jit(solution)/shard_map/ppermute | solution.py:373
  77.8 2.3 %collective-permute-done.27.refs_7_ = bf16[16,1152]{1,0:T(8,128)(2,1)S(1)} collective-permute-done((bf16[16,1152]{1,0:T(8,128)(2,1)S(1)}, bf16[16,1152]{1,0:T(8,128)(2,1)S(1)}, u32[]{:S(2)}, u32[]{:S(2)}) %collective-permute-start.27) | collective-permute-done | bytes 36896 | tf_op jit(solution)/shard_map/ppermute | solution.py:373
  80.2 2.1 %weights.1 = (f32[2,16,4,16,128]{4,3,2,1,0:T(8,128)}, f32[16,16]{1,0:T(8,128)}, f32[1,16]{1,0:T(1,128)}) custom-call(bf16[16,4096]{1,0:T(8,128)(2,1)S(1)} %get-tuple-element.36.refs_0_, bf16[16,4096]{1,0:T(8,128)(2,1)S(1)} %collective-permute-done.22.refs_1_, bf16[16,4096]{1,0:T(8,128)(2,1)S(1)} %collective-permute-done.23.refs_2_, ...), custom_call_target="tpu_custom_call" | custom-call | tf_op jit(solution)/shard_map/weights/pallas_call | solution.py:537
  82.3 0.0 collective-permute-done.20.refs_6_
  82.3 6.9 %field.1 = bf16[16,64,2048]{2,1,0:T(8,128)(2,1)} custom-call(bf16[16,4096]{1,0:T(8,128)(2,1)S(1)} %get-tuple-element.34.refs_0_, bf16[16,4096]{1,0:T(8,128)(2,1)S(1)} %collective-permute-done.15.refs_1_, bf16[16,4096]{1,0:T(8,128)(2,1)S(1)} %collective-permute-done.16.refs_2_, bf16[16,4096]{1,0:T(8,128)(2,1)S(1)} %collective-permute-done.17.refs_3_, ...), custom_call_target="tpu_custom_call" | custom-call | tf_op jit(solution)/shard_map/field/pallas_call | solution.py:573
  (19 shorter events, 0.1 us)
Async XLA Ops:
  0.6 18.0 %copy-start = (bf16[2,16,16,16,128]{4,3,2,1,0:T(8,128)(2,1)S(1)}, bf16[2,16,16,16,128]{4,3,2,1,0:T(8,128)(2,1)}, u32[]{:S(2)}) copy-start(bf16[2,16,16,16,128]{4,3,2,1,0:T(8,128)(2,1)} %weight_ref.3) | copy-start | bytes 6291460
  0.6 28.8 %copy-start.1 = (bf16[16,16]{1,0:T(8,128)(2,1)S(1)}, bf16[16,16]{1,0:T(8,128)(2,1)}, u32[]{:S(2)}) copy-start(bf16[16,16]{1,0:T(8,128)(2,1)} %refs_10_.2) | copy-start | bytes 1540
  0.7 28.8 %copy-start.2 = (f32[16]{0:T(128)S(1)}, f32[16]{0:T(128)}, u32[]{:S(2)}) copy-start(f32[16]{0:T(128)} %param.11) | copy-start | bytes 196
  5.1 2.1 %collective-permute-start = (bf16[64,4096]{1,0:T(8,128)(2,1)S(1)}, bf16[64,4096]{1,0:T(8,128)(2,1)S(1)}, u32[]{:S(2)}, u32[]{:S(2)}) collective-permute-start(bf16[64,4096]{1,0:T(8,128)(2,1)S(1)} %columns.1.mine_ref), channel_id=1, source_target_pairs={{0,1},{1,0},{2,3},{3,2},{4,5},{5,4},{6,7},{7,6},{8,9},{9,8},{10,11... | collective-permute-start | bytes 1572872 | tf_op jit(solution)/shard_map/ppermute | solution.py:373
  7.7 6.9 %collective-permute-start.1 = (bf16[16,4096]{1,0:T(8,128)(2,1)S(1)}, bf16[16,4096]{1,0:T(8,128)(2,1)S(1)}, u32[]{:S(2)}, u32[]{:S(2)}) collective-permute-start(bf16[16,4096]{1,0:T(8,128)(2,1)S(1)} %get-tuple-element.25), channel_id=1, source_target_pairs={{0,2},{1,3},{2,0},{3,1},{4,6},{5,7},{6,4},{7,5},{8,10},{9,11},{10,... | collective-permute-start | bytes 393224 | tf_op jit(solution)/shard_map/ppermute | solution.py:373
  10.6 8.1 %collective-permute-start.2 = (bf16[16,4096]{1,0:T(8,128)(2,1)S(1)}, bf16[16,4096]{1,0:T(8,128)(2,1)S(1)}, u32[]{:S(2)}, u32[]{:S(2)}) collective-permute-start(bf16[16,4096]{1,0:T(8,128)(2,1)S(1)} %get-tuple-element.26), channel_id=1, source_target_pairs={{0,4},{1,5},{2,6},{3,7},{4,0},{5,1},{6,2},{7,3},{8,12},{9,13},{10,... | collective-permute-start | bytes 393224 | tf_op jit(solution)/shard_map/ppermute | solution.py:373
  12.1 6.6 %collective-permute-start.3 = (bf16[16,4096]{1,0:T(8,128)(2,1)S(1)}, bf16[16,4096]{1,0:T(8,128)(2,1)S(1)}, u32[]{:S(2)}, u32[]{:S(2)}) collective-permute-start(bf16[16,4096]{1,0:T(8,128)(2,1)S(1)} %get-tuple-element.27), channel_id=1, source_target_pairs={{0,6},{1,7},{2,4},{3,5},{4,2},{5,3},{6,0},{7,1},{8,14},{9,15},{10,... | collective-permute-start | bytes 393224 | tf_op jit(solution)/shard_map/ppermute | solution.py:373
  19.4 6.0 %collective-permute-start.4 = (bf16[16,4096]{1,0:T(8,128)(2,1)S(1)}, bf16[16,4096]{1,0:T(8,128)(2,1)S(1)}, u32[]{:S(2)}, u32[]{:S(2)}) collective-permute-start(bf16[16,4096]{1,0:T(8,128)(2,1)S(1)} %get-tuple-element.28.refs_0_), channel_id=1, source_target_pairs={{0,2},{1,3},{2,0},{3,1},{4,6},{5,7},{6,4},{7,5},{8,10},{9,11},{10,... | collective-permute-start | bytes 393224 | tf_op jit(solution)/shard_map/ppermute | solution.py:373
  20.7 7.2 %collective-permute-start.5 = (bf16[16,4096]{1,0:T(8,128)(2,1)S(1)}, bf16[16,4096]{1,0:T(8,128)(2,1)S(1)}, u32[]{:S(2)}, u32[]{:S(2)}) collective-permute-start(bf16[16,4096]{1,0:T(8,128)(2,1)S(1)} %get-tuple-element.28.refs_0_), channel_id=1, source_target_pairs={{0,4},{1,5},{2,6},{3,7},{4,0},{5,1},{6,2},{7,3},{8,12},{9,13},{10,... | collective-permute-start | bytes 393224 | tf_op jit(solution)/shard_map/ppermute | solution.py:373
  21.5 6.4 %collective-permute-start.6 = (bf16[16,4096]{1,0:T(8,128)(2,1)S(1)}, bf16[16,4096]{1,0:T(8,128)(2,1)S(1)}, u32[]{:S(2)}, u32[]{:S(2)}) collective-permute-start(bf16[16,4096]{1,0:T(8,128)(2,1)S(1)} %get-tuple-element.28.refs_0_), channel_id=1, source_target_pairs={{0,6},{1,7},{2,4},{3,5},{4,2},{5,3},{6,0},{7,1},{8,14},{9,15},{10,... | collective-permute-start | bytes 393224 | tf_op jit(solution)/shard_map/ppermute | solution.py:373
  23.2 5.5 %collective-permute-start.7 = (bf16[16,4096]{1,0:T(8,128)(2,1)S(1)}, bf16[16,4096]{1,0:T(8,128)(2,1)S(1)}, u32[]{:S(2)}, u32[]{:S(2)}) collective-permute-start(bf16[16,4096]{1,0:T(8,128)(2,1)S(1)} %get-tuple-element.28.refs_0_), channel_id=1, source_target_pairs={{0,1},{1,0},{2,3},{3,2},{4,5},{5,4},{6,7},{7,6},{8,9},{9,8},{10,11... | collective-permute-start | bytes 393224 | tf_op jit(solution)/shard_map/ppermute | solution.py:373
  25.4 3.3 %collective-permute-start.8 = (bf16[16,4096]{1,0:T(8,128)(2,1)S(1)}, bf16[16,4096]{1,0:T(8,128)(2,1)S(1)}, u32[]{:S(2)}, u32[]{:S(2)}) collective-permute-start(bf16[16,4096]{1,0:T(8,128)(2,1)S(1)} %collective-permute-done.4.refs_1_), channel_id=1, source_target_pairs={{0,1},{1,0},{2,3},{3,2},{4,5},{5,4},{6,7},{7,6},{8,9},{9,8},{10,11... | collective-permute-start | bytes 393224 | tf_op jit(solution)/shard_map/ppermute | solution.py:373
  27.9 1.3 %collective-permute-start.9 = (bf16[16,4096]{1,0:T(8,128)(2,1)S(1)}, bf16[16,4096]{1,0:T(8,128)(2,1)S(1)}, u32[]{:S(2)}, u32[]{:S(2)}) collective-permute-start(bf16[16,4096]{1,0:T(8,128)(2,1)S(1)} %collective-permute-done.5.refs_2_), channel_id=1, source_target_pairs={{0,1},{1,0},{2,3},{3,2},{4,5},{5,4},{6,7},{7,6},{8,9},{9,8},{10,11... | collective-permute-start | bytes 393224 | tf_op jit(solution)/shard_map/ppermute | solution.py:373
  27.9 1.5 %collective-permute-start.10 = (bf16[16,4096]{1,0:T(8,128)(2,1)S(1)}, bf16[16,4096]{1,0:T(8,128)(2,1)S(1)}, u32[]{:S(2)}, u32[]{:S(2)}) collective-permute-start(bf16[16,4096]{1,0:T(8,128)(2,1)S(1)} %collective-permute-done.6.refs_3_), channel_id=1, source_target_pairs={{0,1},{1,0},{2,3},{3,2},{4,5},{5,4},{6,7},{7,6},{8,9},{9,8},{10,11... | collective-permute-start | bytes 393224 | tf_op jit(solution)/shard_map/ppermute | solution.py:373
  42.0 1.9 %collective-permute-start.11 = (bf16[64,4224]{1,0:T(8,128)(2,1)S(1)}, bf16[64,4224]{1,0:T(8,128)(2,1)S(1)}, u32[]{:S(2)}, u32[]{:S(2)}) collective-permute-start(bf16[64,4224]{1,0:T(8,128)(2,1)S(1)} %get-tuple-element.29.mine_ref), channel_id=1, source_target_pairs={{0,1},{1,0},{2,3},{3,2},{4,5},{5,4},{6,7},{7,6},{8,9},{9,8},{10,11... | collective-permute-start | bytes 1622024 | tf_op jit(solution)/shard_map/ppermute | solution.py:373
  44.4 7.7 %collective-permute-start.12 = (bf16[16,4224]{1,0:T(8,128)(2,1)S(1)}, bf16[16,4224]{1,0:T(8,128)(2,1)S(1)}, u32[]{:S(2)}, u32[]{:S(2)}) collective-permute-start(bf16[16,4224]{1,0:T(8,128)(2,1)S(1)} %get-tuple-element.31), channel_id=1, source_target_pairs={{0,2},{1,3},{2,0},{3,1},{4,6},{5,7},{6,4},{7,5},{8,10},{9,11},{10,... | collective-permute-start | bytes 405512 | tf_op jit(solution)/shard_map/ppermute | solution.py:373
  45.8 8.4 %collective-permute-start.13 = (bf16[16,4224]{1,0:T(8,128)(2,1)S(1)}, bf16[16,4224]{1,0:T(8,128)(2,1)S(1)}, u32[]{:S(2)}, u32[]{:S(2)}) collective-permute-start(bf16[16,4224]{1,0:T(8,128)(2,1)S(1)} %get-tuple-element.32), channel_id=1, source_target_pairs={{0,4},{1,5},{2,6},{3,7},{4,0},{5,1},{6,2},{7,3},{8,12},{9,13},{10,... | collective-permute-start | bytes 405512 | tf_op jit(solution)/shard_map/ppermute | solution.py:373
  46.6 7.6 %collective-permute-start.14 = (bf16[16,4224]{1,0:T(8,128)(2,1)S(1)}, bf16[16,4224]{1,0:T(8,128)(2,1)S(1)}, u32[]{:S(2)}, u32[]{:S(2)}) collective-permute-start(bf16[16,4224]{1,0:T(8,128)(2,1)S(1)} %get-tuple-element.33), channel_id=1, source_target_pairs={{0,6},{1,7},{2,4},{3,5},{4,2},{5,3},{6,0},{7,1},{8,14},{9,15},{10,... | collective-permute-start | bytes 405512 | tf_op jit(solution)/shard_map/ppermute | solution.py:373
  47.9 10.7 %collective-permute-start.22 = (bf16[16,4096]{1,0:T(8,128)(2,1)S(1)}, bf16[16,4096]{1,0:T(8,128)(2,1)S(1)}, u32[]{:S(2)}, u32[]{:S(2)}) collective-permute-start(bf16[16,4096]{1,0:T(8,128)(2,1)S(1)} %get-tuple-element.36.refs_0_), channel_id=1, source_target_pairs={{0,8},{8,0},{16,24},{24,16},{1,9},{9,1},{17,25},{25,17},{2,10},{10... | collective-permute-start | bytes 393224 | tf_op jit(solution)/shard_map/ppermute | solution.py:373
  49.5 12.7 %collective-permute-start.23 = (bf16[16,4096]{1,0:T(8,128)(2,1)S(1)}, bf16[16,4096]{1,0:T(8,128)(2,1)S(1)}, u32[]{:S(2)}, u32[]{:S(2)}) collective-permute-start(bf16[16,4096]{1,0:T(8,128)(2,1)S(1)} %get-tuple-element.36.refs_0_), channel_id=1, source_target_pairs={{0,16},{8,24},{16,0},{24,8},{1,17},{9,25},{17,1},{25,9},{2,18},{10... | collective-permute-start | bytes 393224 | tf_op jit(solution)/shard_map/ppermute | solution.py:373
  55.0 7.1 %collective-permute-start.15 = (bf16[16,4096]{1,0:T(8,128)(2,1)S(1)}, bf16[16,4096]{1,0:T(8,128)(2,1)S(1)}, u32[]{:S(2)}, u32[]{:S(2)}) collective-permute-start(bf16[16,4096]{1,0:T(8,128)(2,1)S(1)} %get-tuple-element.34.refs_0_), channel_id=1, source_target_pairs={{0,2},{1,3},{2,0},{3,1},{4,6},{5,7},{6,4},{7,5},{8,10},{9,11},{10,... | collective-permute-start | bytes 393224 | tf_op jit(solution)/shard_map/ppermute | solution.py:373
  55.8 7.7 %collective-permute-start.16 = (bf16[16,4096]{1,0:T(8,128)(2,1)S(1)}, bf16[16,4096]{1,0:T(8,128)(2,1)S(1)}, u32[]{:S(2)}, u32[]{:S(2)}) collective-permute-start(bf16[16,4096]{1,0:T(8,128)(2,1)S(1)} %get-tuple-element.34.refs_0_), channel_id=1, source_target_pairs={{0,4},{1,5},{2,6},{3,7},{4,0},{5,1},{6,2},{7,3},{8,12},{9,13},{10,... | collective-permute-start | bytes 393224 | tf_op jit(solution)/shard_map/ppermute | solution.py:373
  57.1 6.4 %collective-permute-start.17 = (bf16[16,4096]{1,0:T(8,128)(2,1)S(1)}, bf16[16,4096]{1,0:T(8,128)(2,1)S(1)}, u32[]{:S(2)}, u32[]{:S(2)}) collective-permute-start(bf16[16,4096]{1,0:T(8,128)(2,1)S(1)} %get-tuple-element.34.refs_0_), channel_id=1, source_target_pairs={{0,6},{1,7},{2,4},{3,5},{4,2},{5,3},{6,0},{7,1},{8,14},{9,15},{10,... | collective-permute-start | bytes 393224 | tf_op jit(solution)/shard_map/ppermute | solution.py:373
  58.6 6.9 %collective-permute-start.24 = (bf16[16,4096]{1,0:T(8,128)(2,1)S(1)}, bf16[16,4096]{1,0:T(8,128)(2,1)S(1)}, u32[]{:S(2)}, u32[]{:S(2)}) collective-permute-start(bf16[16,4096]{1,0:T(8,128)(2,1)S(1)} %get-tuple-element.36.refs_0_), channel_id=1, source_target_pairs={{0,24},{8,16},{16,8},{24,0},{1,25},{9,17},{17,9},{25,1},{2,26},{10... | collective-permute-start | bytes 393224 | tf_op jit(solution)/shard_map/ppermute | solution.py:373
  62.2 20.1 %collective-permute-start.18 = (bf16[16,4096]{1,0:T(8,128)(2,1)S(1)}, bf16[16,4096]{1,0:T(8,128)(2,1)S(1)}, u32[]{:S(2)}, u32[]{:S(2)}) collective-permute-start(bf16[16,4096]{1,0:T(8,128)(2,1)S(1)} %get-tuple-element.34.refs_0_), channel_id=1, source_target_pairs={{0,1},{1,0},{2,3},{3,2},{4,5},{5,4},{6,7},{7,6},{8,9},{9,8},{10,11... | collective-permute-start | bytes 393224 | tf_op jit(solution)/shard_map/ppermute | solution.py:373
  62.2 20.1 %collective-permute-start.19 = (bf16[16,4096]{1,0:T(8,128)(2,1)S(1)}, bf16[16,4096]{1,0:T(8,128)(2,1)S(1)}, u32[]{:S(2)}, u32[]{:S(2)}) collective-permute-start(bf16[16,4096]{1,0:T(8,128)(2,1)S(1)} %collective-permute-done.15.refs_1_), channel_id=1, source_target_pairs={{0,1},{1,0},{2,3},{3,2},{4,5},{5,4},{6,7},{7,6},{8,9},{9,8},{10,11... | collective-permute-start | bytes 393224 | tf_op jit(solution)/shard_map/ppermute | solution.py:373
  63.6 18.7 %collective-permute-start.20 = (bf16[16,4096]{1,0:T(8,128)(2,1)S(1)}, bf16[16,4096]{1,0:T(8,128)(2,1)S(1)}, u32[]{:S(2)}, u32[]{:S(2)}) collective-permute-start(bf16[16,4096]{1,0:T(8,128)(2,1)S(1)} %collective-permute-done.16.refs_2_), channel_id=1, source_target_pairs={{0,1},{1,0},{2,3},{3,2},{4,5},{5,4},{6,7},{7,6},{8,9},{9,8},{10,11... | collective-permute-start | bytes 393224 | tf_op jit(solution)/shard_map/ppermute | solution.py:373
  63.6 18.7 %collective-permute-start.21 = (bf16[16,4096]{1,0:T(8,128)(2,1)S(1)}, bf16[16,4096]{1,0:T(8,128)(2,1)S(1)}, u32[]{:S(2)}, u32[]{:S(2)}) collective-permute-start(bf16[16,4096]{1,0:T(8,128)(2,1)S(1)} %collective-permute-done.17.refs_3_), channel_id=1, source_target_pairs={{0,1},{1,0},{2,3},{3,2},{4,5},{5,4},{6,7},{7,6},{8,9},{9,8},{10,11... | collective-permute-start | bytes 393224 | tf_op jit(solution)/shard_map/ppermute | solution.py:373
  65.5 4.0 %collective-permute-start.25 = (bf16[16,1152]{1,0:T(8,128)(2,1)S(1)}, bf16[16,1152]{1,0:T(8,128)(2,1)S(1)}, u32[]{:S(2)}, u32[]{:S(2)}) collective-permute-start(bf16[16,1152]{1,0:T(8,128)(2,1)S(1)} %get-tuple-element.38), channel_id=1, source_target_pairs={{0,8},{8,0},{16,24},{24,16},{1,9},{9,1},{17,25},{25,17},{2,10},{10... | collective-permute-start | bytes 110600 | tf_op jit(solution)/shard_map/ppermute | solution.py:373
  69.4 5.0 %collective-permute-start.26 = (bf16[16,1152]{1,0:T(8,128)(2,1)S(1)}, bf16[16,1152]{1,0:T(8,128)(2,1)S(1)}, u32[]{:S(2)}, u32[]{:S(2)}) collective-permute-start(bf16[16,1152]{1,0:T(8,128)(2,1)S(1)} %get-tuple-element.39), channel_id=1, source_target_pairs={{0,16},{8,24},{16,0},{24,8},{1,17},{9,25},{17,1},{25,9},{2,18},{10... | collective-permute-start | bytes 110600 | tf_op jit(solution)/shard_map/ppermute | solution.py:373
  74.4 5.8 %collective-permute-start.27 = (bf16[16,1152]{1,0:T(8,128)(2,1)S(1)}, bf16[16,1152]{1,0:T(8,128)(2,1)S(1)}, u32[]{:S(2)}, u32[]{:S(2)}) collective-permute-start(bf16[16,1152]{1,0:T(8,128)(2,1)S(1)} %get-tuple-element.40), channel_id=1, source_target_pairs={{0,24},{8,16},{16,8},{24,0},{1,25},{9,17},{17,9},{25,1},{2,26},{10... | collective-permute-start | bytes 110600 | tf_op jit(solution)/shard_map/ppermute | solution.py:373
where the time goes:
time: 89.5 us; the launch traced here: 89.2 us
  starting transfers between devices  33 us (37%)
  Pallas kernels  28.5 us (32%)
  waiting for transfers between devices  26 us (29%)
    ppermute x28, starting transfers between devices, swap(): return lax.ppermute(value, axis, [(at, at ^ mask) for at in range(size)])  33 us
    ppermute x28, waiting for transfers between devices, swap(): return lax.ppermute(value, axis, [(at, at ^ mask) for at in range(size)])  26 us
    pallas_call x1, Pallas kernels, on_device(): main(*mixed, to_rows, streamed(inverse), streamed(forward), local_weight,...  12.6 us
    pallas_call x1, Pallas kernels, on_device(): final(*freq_grad, to_rows, streamed(inverse), local_weight, streamed(grad...  6.92 us
    pallas_call x1, Pallas kernels, on_device(): pl.pallas_call(columns_kernel, name='columns', grid=(tiles,), in_specs=[b...  4.46 us
    pallas_call x1, Pallas kernels, on_device(): pl.pallas_call(functools.partial(weight_kernel, chans, modes, map_count,...  2.13 us
  transfers between devices with their start and end apart: 28, of which 14 were waited for; matrix products, arithmetic and copies ran while one was open for 1% of the time, Pallas kernels for 3%

commit v1 on v0

--- a/solution.py
+++ b/solution.py
@@ -13,7 +13,8 @@
 BF16 = jnp.bfloat16
 F32 = jnp.float32
 LANES = 128
-TILE = 512
+TILE = 1024
+MAIN_TILE = 512
 GROUP = 16
 
 
@@ -269,10 +270,12 @@
     for o in range(chans):
         at = slice(o * lanes, (o + 1) * lanes)
         part = dot(phase, jnp.concatenate([chunk[:, at] for chunk in chunks], axis=0))
-        real = (part[:half, :modes] - part[half:, modes:]) * factor
-        imag = (part[:half, modes:] + part[half:, :modes]) * factor
-        out[o * half : (o + 1) * half, :modes] = real.astype(BF16)
-        out[o * half : (o + 1) * half, modes:] = imag.astype(BF16)
+        real = ((part[:half, :modes] - part[half:, modes:]) * factor).astype(BF16)
+        imag = ((part[:half, modes:] + part[half:, :modes]) * factor).astype(BF16)
+        for at in range(0, half, GROUP):
+            first = at * chans + o * GROUP
+            out[first : first + GROUP, :modes] = real[at : at + GROUP]
+            out[first : first + GROUP, modes:] = imag[at : at + GROUP]
 
 
 SLOPE = math.sqrt(2.0 / math.pi)
@@ -293,7 +296,7 @@
     (phase_ref, inverse_ref, forward_ref, local_ref, bias_ref, field_ref, cot_ref) = refs[
         count : count + 7
     ]
-    grad_ref, sums_ref, rows, mixer, wide, total, outer = refs[count + 7 :]
+    grad_ref, sums_ref, rows, mixer, total, outer = refs[count + 7 :]
     step = pl.program_id(0)
     size = chans * GROUP
     here, tile = field_ref.shape[1:]
@@ -311,12 +314,12 @@
     group = lax.broadcasted_iota(jnp.int32, (size, chans), 0) // GROUP
     pick = group == lax.broadcasted_iota(jnp.int32, (size, chans), 1)
     bias = jnp.sum(jnp.where(pick, bias_ref[...], 0.0), axis=1, keepdims=True)
-    wide[...] = dot(rows[...], inverse_ref[...]).reshape(chans, here, tile)
     both = jnp.zeros((size, size), F32)
     for at in range(0, here, GROUP):
         block = slice(at, at + GROUP)
+        mine = rows[at * chans : (at + GROUP) * chans]
         field = field_ref[:, block, :].reshape(size, tile)
-        preact = dot(mix, field) + wide[:, block, :].reshape(size, tile) + bias
+        preact = dot(mix, field) + dot(mine, inverse_ref[...]) + bias
         cot = cot_ref[:, block, :].reshape(size, tile)
         grad = cot * gelu_slope(preact.astype(BF16))
         grad_ref[:, block, :] = grad.reshape(chans, GROUP, tile)
@@ -350,7 +353,7 @@
 
 def field_kernel(chans, modes, scale, count, *refs):
     chunks = refs[:count]
-    phase_ref, inverse_ref, local_ref, grad_ref, out_ref, rows, mixer, wide = refs[count:]
+    phase_ref, inverse_ref, local_ref, grad_ref, out_ref, rows, mixer = refs[count:]
     size = chans * GROUP
     here, tile = grad_ref.shape[1:]
 
@@ -360,11 +363,10 @@
         mixer[...] = channel_map(local_ref, chans, True)
 
     mix = mixer[...]
-    wide[...] = dot(rows[...], inverse_ref[...]).reshape(chans, here, tile)
     for at in range(0, here, GROUP):
         block = slice(at, at + GROUP)
-        value = dot(mix, grad_ref[:, block, :].reshape(size, tile))
-        value = value + wide[:, block, :].reshape(size, tile)
+        mine = rows[at * chans : (at + GROUP) * chans]
+        value = dot(mix, grad_ref[:, block, :].reshape(size, tile)) + dot(mine, inverse_ref[...])
         out_ref[:, block, :] = value.astype(BF16).reshape(chans, GROUP, tile)
 
 
@@ -409,11 +411,18 @@
     angle = row_angles(all_modes, me * rows_here + here, height, modes).T
     to_rows = jnp.concatenate([jnp.cos(angle), jnp.sin(angle)], axis=0).astype(BF16)
 
-    tile = min(TILE, width)
-    tiles = width // tile
-    block = pl.BlockSpec((chans, rows_here, tile), lambda i: (0, 0, i))
-    inverse_block = pl.BlockSpec((lanes, tile), lambda i: (0, i))
-    forward_block = pl.BlockSpec((tile, lanes), lambda i: (i, 0))
+
+    def blocks(most):
+        tile = min(most, width)
+        return (
+            width // tile,
+            pl.BlockSpec((chans, rows_here, tile), lambda i: (0, 0, i)),
+            pl.BlockSpec((lanes, tile), lambda i: (0, i)),
+            pl.BlockSpec((tile, lanes), lambda i: (i, 0)),
+        )
+
+    tiles, block, inverse_block, forward_block = blocks(TILE)
+    main_tiles, main_block, main_inverse, main_forward = blocks(MAIN_TILE)
 
     def rows_step(mine, other, more):
         out_lanes = flat + (extra if more else 0)
@@ -452,11 +461,14 @@
             kernel, name="small", out_shape=jax.ShapeDtypeStruct((chans, LANES), BF16)
         )(mine, other)
 
-    def spread(pieces):
-        return [pieces[0]] + [swap(pieces[d], "row", 2 * d) for d in range(1, chips)]
+    def across_chips(pieces):
+        came = [pieces[0]]
+        for d in range(1, chips):
+            came.append(swap(pieces[d], "row", 2 * d))
+        return came
 
     def gather(piece):
-        same = [piece] + [swap(piece, "row", 2 * d) for d in range(1, chips)]
+        same = across_chips([piece] * chips)
         chunks = same + [swap(part, "row", 1) for part in same]
         return chunks if aligned else [jnp.concatenate(chunks, axis=0)]
 
@@ -470,7 +482,7 @@
         scratch_shapes=[pltpu.VMEM((chans * rows_here, lanes), F32)],
         compiler_params=room(12),
     )(streamed(field), streamed(forward))
-    chunks = spread(rows_step(coeffs, swap(coeffs, "row", 1), False))
+    chunks = across_chips(rows_step(coeffs, swap(coeffs, "row", 1), False))
 
     mixed, spectrum = pl.pallas_call(
         functools.partial(mix_kernel, chans, modes, chips),
@@ -486,18 +498,18 @@
     main = pl.pallas_call(
         functools.partial(main_kernel, chans, modes, scale, len(mixed)),
         name="main",
-        grid=(tiles,),
+        grid=(main_tiles,),
         in_specs=chunk_specs
         + [
             whole(to_rows.shape),
-            inverse_block,
-            forward_block,
+            main_inverse,
+            main_forward,
             whole((chans, chans)),
             whole((1, chans)),
-            block,
-            block,
-        ],
-        out_specs=[block, whole((rows_here, flat + LANES))],
+            main_block,
+            main_block,
+        ],
+        out_specs=[main_block, whole((rows_here, flat + LANES))],
         out_shape=[
             pltpu.HBM(field.shape, BF16),
             jax.ShapeDtypeStruct((rows_here, flat + LANES), BF16),
@@ -505,7 +517,6 @@
         scratch_shapes=[
             pltpu.VMEM((chans * rows_here, lanes), BF16),
             pltpu.VMEM((size, size), BF16),
-            pltpu.VMEM((chans, rows_here, tile), F32),
             pltpu.VMEM((chans * rows_here, lanes), F32),
             pltpu.VMEM((size, size), F32),
         ],
@@ -515,7 +526,7 @@
         *mixed, to_rows, streamed(inverse), streamed(forward), local_weight, bias[None], streamed(field), streamed(cot)
     )
 
-    chunks = spread(rows_step(grad_coeffs, swap(grad_coeffs, "row", 1), True))
+    chunks = across_chips(rows_step(grad_coeffs, swap(grad_coeffs, "row", 1), True))
     part_lanes = chans // map_count * lanes
     outs = pl.pallas_call(
         functools.partial(back_kernel, chans, modes, chips, map_count),
@@ -533,7 +544,7 @@
     freq_grad = gather(outs[0])
     slices = [outs[1]] + [swap(outs[1 + d], "dp", d) for d in range(1, map_count)]
 
-    steps = 4 if chans % 4 == 0 else 1
+    steps = 1
     spectral_grad, local_grad, bias_grad = pl.pallas_call(
         functools.partial(weight_kernel, chans, modes, map_count, grad_scale),
         name="weights",
@@ -566,7 +577,6 @@
         scratch_shapes=[
             pltpu.VMEM((chans * rows_here, lanes), BF16),
             pltpu.VMEM((size, size), BF16),
-            pltpu.VMEM((chans, rows_here, tile), F32),
         ],
         compiler_params=room(20),
     )

time: 89.5 us -> 85.6 us (0.956)
  Pallas kernels: 28.5 us -> 24.6 us
    pallas_call x1, Pallas kernels: 12.6 us -> 10.7 us  [on_device(): main(*mixed, to_rows, streamed(inverse), streamed(forward), local_weight,...]
    pallas_call x1, Pallas kernels: 4.46 us -> 3.5 us  [on_device(): pl.pallas_call(columns_kernel, name='columns', grid=(tiles,), in_specs=[b...]
where the time goes in v1:
time: 85.6 us; the launch traced here: 85.4 us
  starting transfers between devices  33.2 us (39%)
  waiting for transfers between devices  25.9 us (30%)
  Pallas kernels  24.6 us (29%)
    ppermute x28, starting transfers between devices, swap(): return lax.ppermute(value, axis, [(at, at ^ mask) for at in range(size)])  33.2 us
    ppermute x28, waiting for transfers between devices, swap(): return lax.ppermute(value, axis, [(at, at ^ mask) for at in range(size)])  25.9 us
    pallas_call x1, Pallas kernels, on_device(): main(*mixed, to_rows, streamed(inverse), streamed(forward), local_weight,...  10.7 us
    pallas_call x1, Pallas kernels, on_device(): final(*freq_grad, to_rows, streamed(inverse), local_weight, streamed(grad...  6.28 us
    pallas_call x1, Pallas kernels, on_device(): pl.pallas_call(columns_kernel, name='columns', grid=(tiles,), in_specs=[b...  3.5 us
  transfers between devices with their start and end apart: 28, of which 14 were waited for; matrix products, arithmetic and copies ran while one was open for 1% of the time, Pallas kernels for 3%

profile of v1, /device:TPU:0, one launch (start us, length us, event | category | flops | bytes accessed | tf_op | source)
XLA Modules:
  0.0 85.4 jit_solution(10739883548613920821)
XLA Ops:
  0.7 3.5 %columns.1.mine_ref = bf16[64,4096]{1,0:T(8,128)(2,1)S(1)} custom-call(bf16[16,64,2048]{2,1,0:T(8,128)(2,1)} %bitcast.7, bf16[2048,256]{1,0:T(8,128)(2,1)} %constant.90.clone.table_ref.refs_10_), custom_call_target="tpu_custom_call" | custom-call | tf_op jit(solution)/shard_map/columns/pallas_call | solution.py:475
  4.2 0.6 collective-permute-start
  4.7 0.1 iota_add_fusion.1
  4.8 0.1 add.131
  4.9 0.1 pad_add_fusion
  5.0 0.2 cosine_convert_fusion.1
  5.2 1.0 %collective-permute-done.other_ref = bf16[64,4096]{1,0:T(8,128)(2,1)S(1)} collective-permute-done((bf16[64,4096]{1,0:T(8,128)(2,1)S(1)}, bf16[64,4096]{1,0:T(8,128)(2,1)S(1)}, u32[]{:S(2)}, u32[]{:S(2)}) %collective-permute-start) | collective-permute-done | bytes 524320 | tf_op jit(solution)/shard_map/ppermute | solution.py:375
  6.3 0.4 rows.2
  6.7 2.9 %collective-permute-start.1 = (bf16[16,4096]{1,0:T(8,128)(2,1)S(1)}, bf16[16,4096]{1,0:T(8,128)(2,1)S(1)}, u32[]{:S(2)}, u32[]{:S(2)}) collective-permute-start(bf16[16,4096]{1,0:T(8,128)(2,1)S(1)} %get-tuple-element.25), channel_id=1, source_target_pairs={{0,2},{1,3},{2,0},{3,1},{4,6},{5,7},{6,4},{7,5},{8,10},{9,11},{10,... | collective-permute-start | bytes 393224 | tf_op jit(solution)/shard_map/ppermute | solution.py:375
  9.6 1.5 %collective-permute-start.2 = (bf16[16,4096]{1,0:T(8,128)(2,1)S(1)}, bf16[16,4096]{1,0:T(8,128)(2,1)S(1)}, u32[]{:S(2)}, u32[]{:S(2)}) collective-permute-start(bf16[16,4096]{1,0:T(8,128)(2,1)S(1)} %get-tuple-element.26), channel_id=1, source_target_pairs={{0,4},{1,5},{2,6},{3,7},{4,0},{5,1},{6,2},{7,3},{8,12},{9,13},{10,... | collective-permute-start | bytes 393224 | tf_op jit(solution)/shard_map/ppermute | solution.py:375
  11.1 0.0 collective-permute-start.3
  11.1 2.4 %collective-permute-done.1.refs_1_ = bf16[16,4096]{1,0:T(8,128)(2,1)S(1)} collective-permute-done((bf16[16,4096]{1,0:T(8,128)(2,1)S(1)}, bf16[16,4096]{1,0:T(8,128)(2,1)S(1)}, u32[]{:S(2)}, u32[]{:S(2)}) %collective-permute-start.1) | collective-permute-done | bytes 131104 | tf_op jit(solution)/shard_map/ppermute | solution.py:375
  13.6 4.1 %collective-permute-done.2.refs_2_ = bf16[16,4096]{1,0:T(8,128)(2,1)S(1)} collective-permute-done((bf16[16,4096]{1,0:T(8,128)(2,1)S(1)}, bf16[16,4096]{1,0:T(8,128)(2,1)S(1)}, u32[]{:S(2)}, u32[]{:S(2)}) %collective-permute-start.2) | collective-permute-done | bytes 131104 | tf_op jit(solution)/shard_map/ppermute | solution.py:375
  17.7 0.0 collective-permute-done.3.refs_3_
  17.7 0.7 mix.1
  18.4 1.3 %collective-permute-start.4 = (bf16[16,4096]{1,0:T(8,128)(2,1)S(1)}, bf16[16,4096]{1,0:T(8,128)(2,1)S(1)}, u32[]{:S(2)}, u32[]{:S(2)}) collective-permute-start(bf16[16,4096]{1,0:T(8,128)(2,1)S(1)} %get-tuple-element.28.refs_0_), channel_id=1, source_target_pairs={{0,2},{1,3},{2,0},{3,1},{4,6},{5,7},{6,4},{7,5},{8,10},{9,11},{10,... | collective-permute-start | bytes 393224 | tf_op jit(solution)/shard_map/ppermute | solution.py:375
  19.7 0.8 collective-permute-start.5
  20.5 1.4 %collective-permute-start.6 = (bf16[16,4096]{1,0:T(8,128)(2,1)S(1)}, bf16[16,4096]{1,0:T(8,128)(2,1)S(1)}, u32[]{:S(2)}, u32[]{:S(2)}) collective-permute-start(bf16[16,4096]{1,0:T(8,128)(2,1)S(1)} %get-tuple-element.28.refs_0_), channel_id=1, source_target_pairs={{0,6},{1,7},{2,4},{3,5},{4,2},{5,3},{6,0},{7,1},{8,14},{9,15},{10,... | collective-permute-start | bytes 393224 | tf_op jit(solution)/shard_map/ppermute | solution.py:375
  22.0 0.1 iota_add_fusion
  22.0 0.1 add.142
  22.1 0.1 and_select_fusion
  22.2 0.0 collective-permute-start.7
  22.2 2.2 %collective-permute-done.4.refs_1_ = bf16[16,4096]{1,0:T(8,128)(2,1)S(1)} collective-permute-done((bf16[16,4096]{1,0:T(8,128)(2,1)S(1)}, bf16[16,4096]{1,0:T(8,128)(2,1)S(1)}, u32[]{:S(2)}, u32[]{:S(2)}) %collective-permute-start.4) | collective-permute-done | bytes 131104 | tf_op jit(solution)/shard_map/ppermute | solution.py:375
  24.4 0.0 collective-permute-start.8
  24.4 2.5 %collective-permute-done.5.refs_2_ = bf16[16,4096]{1,0:T(8,128)(2,1)S(1)} collective-permute-done((bf16[16,4096]{1,0:T(8,128)(2,1)S(1)}, bf16[16,4096]{1,0:T(8,128)(2,1)S(1)}, u32[]{:S(2)}, u32[]{:S(2)}) %collective-permute-start.5) | collective-permute-done | bytes 131104 | tf_op jit(solution)/shard_map/ppermute | solution.py:375
  26.9 0.0 collective-permute-start.9
  26.9 0.0 collective-permute-done.6.refs_3_
  26.9 0.5 collective-permute-start.10
  27.5 0.2 cosine_convert_fusion
  27.7 0.0 collective-permute-done.7.refs_4_
  27.7 0.6 collective-permute-done.9.refs_6_
  28.3 0.2 collective-permute-done.10.refs_7_
  28.5 10.7 %main.1 = (bf16[16,64,2048]{2,1,0:T(8,128)(2,1)}, bf16[64,4224]{1,0:T(8,128)(2,1)S(1)}) custom-call(bf16[16,4096]{1,0:T(8,128)(2,1)S(1)} %get-tuple-element.28.refs_0_, bf16[16,4096]{1,0:T(8,128)(2,1)S(1)} %collective-permute-done.4.refs_1_, bf16[16,4096]{1,0:T(8,128)(2,1)S(1)} %collective-permute-done.5.refs_2_, ...), custom_call_target="tpu_custom_call" | custom-call | tf_op jit(solution)/shard_map/main/pallas_call | solution.py:525
  39.2 0.3 collective-permute-start.11
  39.5 1.6 %collective-permute-done.11.other_ref = bf16[64,4224]{1,0:T(8,128)(2,1)S(1)} collective-permute-done((bf16[64,4224]{1,0:T(8,128)(2,1)S(1)}, bf16[64,4224]{1,0:T(8,128)(2,1)S(1)}, u32[]{:S(2)}, u32[]{:S(2)}) %collective-permute-start.11) | collective-permute-done | bytes 540704 | tf_op jit(solution)/shard_map/ppermute | solution.py:375
  41.1 0.4 rows.3
  41.6 1.4 %collective-permute-start.12 = (bf16[16,4224]{1,0:T(8,128)(2,1)S(1)}, bf16[16,4224]{1,0:T(8,128)(2,1)S(1)}, u32[]{:S(2)}, u32[]{:S(2)}) collective-permute-start(bf16[16,4224]{1,0:T(8,128)(2,1)S(1)} %get-tuple-element.31), channel_id=1, source_target_pairs={{0,2},{1,3},{2,0},{3,1},{4,6},{5,7},{6,4},{7,5},{8,10},{9,11},{10,... | collective-permute-start | bytes 405512 | tf_op jit(solution)/shard_map/ppermute | solution.py:375
  42.9 0.9 %collective-permute-start.13 = (bf16[16,4224]{1,0:T(8,128)(2,1)S(1)}, bf16[16,4224]{1,0:T(8,128)(2,1)S(1)}, u32[]{:S(2)}, u32[]{:S(2)}) collective-permute-start(bf16[16,4224]{1,0:T(8,128)(2,1)S(1)} %get-tuple-element.32), channel_id=1, source_target_pairs={{0,4},{1,5},{2,6},{3,7},{4,0},{5,1},{6,2},{7,3},{8,12},{9,13},{10,... | collective-permute-start | bytes 405512 | tf_op jit(solution)/shard_map/ppermute | solution.py:375
  43.8 1.3 %collective-permute-start.14 = (bf16[16,4224]{1,0:T(8,128)(2,1)S(1)}, bf16[16,4224]{1,0:T(8,128)(2,1)S(1)}, u32[]{:S(2)}, u32[]{:S(2)}) collective-permute-start(bf16[16,4224]{1,0:T(8,128)(2,1)S(1)} %get-tuple-element.33), channel_id=1, source_target_pairs={{0,6},{1,7},{2,4},{3,5},{4,2},{5,3},{6,0},{7,1},{8,14},{9,15},{10,... | collective-permute-start | bytes 405512 | tf_op jit(solution)/shard_map/ppermute | solution.py:375
  45.1 1.6 %collective-permute-start.22 = (bf16[16,4096]{1,0:T(8,128)(2,1)S(1)}, bf16[16,4096]{1,0:T(8,128)(2,1)S(1)}, u32[]{:S(2)}, u32[]{:S(2)}) collective-permute-start(bf16[16,4096]{1,0:T(8,128)(2,1)S(1)} %get-tuple-element.36.refs_0_), channel_id=1, source_target_pairs={{0,8},{8,0},{16,24},{24,16},{1,9},{9,1},{17,25},{25,17},{2,10},{10... | collective-permute-start | bytes 393224 | tf_op jit(solution)/shard_map/ppermute | solution.py:375
  46.7 2.6 %collective-permute-start.23 = (bf16[16,4096]{1,0:T(8,128)(2,1)S(1)}, bf16[16,4096]{1,0:T(8,128)(2,1)S(1)}, u32[]{:S(2)}, u32[]{:S(2)}) collective-permute-start(bf16[16,4096]{1,0:T(8,128)(2,1)S(1)} %get-tuple-element.36.refs_0_), channel_id=1, source_target_pairs={{0,16},{8,24},{16,0},{24,8},{1,17},{9,25},{17,1},{25,9},{2,18},{10... | collective-permute-start | bytes 393224 | tf_op jit(solution)/shard_map/ppermute | solution.py:375
  49.3 2.1 %collective-permute-done.13.refs_2_ = bf16[16,4224]{1,0:T(8,128)(2,1)S(1)} collective-permute-done((bf16[16,4224]{1,0:T(8,128)(2,1)S(1)}, bf16[16,4224]{1,0:T(8,128)(2,1)S(1)}, u32[]{:S(2)}, u32[]{:S(2)}) %collective-permute-start.13) | collective-permute-done | bytes 135200 | tf_op jit(solution)/shard_map/ppermute | solution.py:375
  51.4 0.0 collective-permute-done.14.refs_3_
  51.4 0.8 back.1
  52.2 0.8 collective-permute-start.15
  53.0 1.3 %collective-permute-start.16 = (bf16[16,4096]{1,0:T(8,128)(2,1)S(1)}, bf16[16,4096]{1,0:T(8,128)(2,1)S(1)}, u32[]{:S(2)}, u32[]{:S(2)}) collective-permute-start(bf16[16,4096]{1,0:T(8,128)(2,1)S(1)} %get-tuple-element.34.refs_0_), channel_id=1, source_target_pairs={{0,4},{1,5},{2,6},{3,7},{4,0},{5,1},{6,2},{7,3},{8,12},{9,13},{10,... | collective-permute-start | bytes 393224 | tf_op jit(solution)/shard_map/ppermute | solution.py:375
  54.3 1.4 %collective-permute-start.17 = (bf16[16,4096]{1,0:T(8,128)(2,1)S(1)}, bf16[16,4096]{1,0:T(8,128)(2,1)S(1)}, u32[]{:S(2)}, u32[]{:S(2)}) collective-permute-start(bf16[16,4096]{1,0:T(8,128)(2,1)S(1)} %get-tuple-element.34.refs_0_), channel_id=1, source_target_pairs={{0,6},{1,7},{2,4},{3,5},{4,2},{5,3},{6,0},{7,1},{8,14},{9,15},{10,... | collective-permute-start | bytes 393224 | tf_op jit(solution)/shard_map/ppermute | solution.py:375
  55.8 3.6 %collective-permute-start.24 = (bf16[16,4096]{1,0:T(8,128)(2,1)S(1)}, bf16[16,4096]{1,0:T(8,128)(2,1)S(1)}, u32[]{:S(2)}, u32[]{:S(2)}) collective-permute-start(bf16[16,4096]{1,0:T(8,128)(2,1)S(1)} %get-tuple-element.36.refs_0_), channel_id=1, source_target_pairs={{0,24},{8,16},{16,8},{24,0},{1,25},{9,17},{17,9},{25,1},{2,26},{10... | collective-permute-start | bytes 393224 | tf_op jit(solution)/shard_map/ppermute | solution.py:375
  59.4 0.0 collective-permute-start.18
  59.4 0.0 collective-permute-done.15.refs_1_
  59.4 0.5 collective-permute-start.19
  59.9 0.8 collective-permute-done.16.refs_2_
  60.7 0.5 collective-permute-start.21
  61.2 1.4 %collective-permute-done.24.refs_3_ = bf16[16,4096]{1,0:T(8,128)(2,1)S(1)} collective-permute-done((bf16[16,4096]{1,0:T(8,128)(2,1)S(1)}, bf16[16,4096]{1,0:T(8,128)(2,1)S(1)}, u32[]{:S(2)}, u32[]{:S(2)}) %collective-permute-start.24) | collective-permute-done | bytes 131104 | tf_op jit(solution)/shard_map/ppermute | solution.py:375
  62.6 1.3 %collective-permute-start.25 = (bf16[16,1152]{1,0:T(8,128)(2,1)S(1)}, bf16[16,1152]{1,0:T(8,128)(2,1)S(1)}, u32[]{:S(2)}, u32[]{:S(2)}) collective-permute-start(bf16[16,1152]{1,0:T(8,128)(2,1)S(1)} %get-tuple-element.38), channel_id=1, source_target_pairs={{0,8},{8,0},{16,24},{24,16},{1,9},{9,1},{17,25},{25,17},{2,10},{10... | collective-permute-start | bytes 110600 | tf_op jit(solution)/shard_map/ppermute | solution.py:375
  63.9 2.7 %collective-permute-done.25.refs_5_ = bf16[16,1152]{1,0:T(8,128)(2,1)S(1)} collective-permute-done((bf16[16,1152]{1,0:T(8,128)(2,1)S(1)}, bf16[16,1152]{1,0:T(8,128)(2,1)S(1)}, u32[]{:S(2)}, u32[]{:S(2)}) %collective-permute-start.25) | collective-permute-done | bytes 36896 | tf_op jit(solution)/shard_map/ppermute | solution.py:375
  66.6 3.1 %collective-permute-start.26 = (bf16[16,1152]{1,0:T(8,128)(2,1)S(1)}, bf16[16,1152]{1,0:T(8,128)(2,1)S(1)}, u32[]{:S(2)}, u32[]{:S(2)}) collective-permute-start(bf16[16,1152]{1,0:T(8,128)(2,1)S(1)} %get-tuple-element.39), channel_id=1, source_target_pairs={{0,16},{8,24},{16,0},{24,8},{1,17},{9,25},{17,1},{25,9},{2,18},{10... | collective-permute-start | bytes 110600 | tf_op jit(solution)/shard_map/ppermute | solution.py:375
  69.7 1.9 %collective-permute-done.26.refs_6_ = bf16[16,1152]{1,0:T(8,128)(2,1)S(1)} collective-permute-done((bf16[16,1152]{1,0:T(8,128)(2,1)S(1)}, bf16[16,1152]{1,0:T(8,128)(2,1)S(1)}, u32[]{:S(2)}, u32[]{:S(2)}) %collective-permute-start.26) | collective-permute-done | bytes 36896 | tf_op jit(solution)/shard_map/ppermute | solution.py:375
  71.6 3.5 %collective-permute-start.27 = (bf16[16,1152]{1,0:T(8,128)(2,1)S(1)}, bf16[16,1152]{1,0:T(8,128)(2,1)S(1)}, u32[]{:S(2)}, u32[]{:S(2)}) collective-permute-start(bf16[16,1152]{1,0:T(8,128)(2,1)S(1)} %get-tuple-element.40), channel_id=1, source_target_pairs={{0,24},{8,16},{16,8},{24,0},{1,25},{9,17},{17,9},{25,1},{2,26},{10... | collective-permute-start | bytes 110600 | tf_op jit(solution)/shard_map/ppermute | solution.py:375
  75.1 2.3 %collective-permute-done.27.refs_7_ = bf16[16,1152]{1,0:T(8,128)(2,1)S(1)} collective-permute-done((bf16[16,1152]{1,0:T(8,128)(2,1)S(1)}, bf16[16,1152]{1,0:T(8,128)(2,1)S(1)}, u32[]{:S(2)}, u32[]{:S(2)}) %collective-permute-start.27) | collective-permute-done | bytes 36896 | tf_op jit(solution)/shard_map/ppermute | solution.py:375
  77.4 1.7 %weights.1 = (f32[2,16,4,16,128]{4,3,2,1,0:T(8,128)}, f32[16,16]{1,0:T(8,128)}, f32[1,16]{1,0:T(1,128)}) custom-call(bf16[16,4096]{1,0:T(8,128)(2,1)S(1)} %get-tuple-element.36.refs_0_, bf16[16,4096]{1,0:T(8,128)(2,1)S(1)} %collective-permute-done.22.refs_1_, bf16[16,4096]{1,0:T(8,128)(2,1)S(1)} %collective-permute-done.23.refs_2_, ...), custom_call_target="tpu_custom_call" | custom-call | tf_op jit(solution)/shard_map/weights/pallas_call | solution.py:548
  79.1 0.0 collective-permute-done.18.refs_4_
  79.1 0.0 collective-permute-done.19.refs_5_
  79.1 6.3 %field.1 = bf16[16,64,2048]{2,1,0:T(8,128)(2,1)} custom-call(bf16[16,4096]{1,0:T(8,128)(2,1)S(1)} %get-tuple-element.34.refs_0_, bf16[16,4096]{1,0:T(8,128)(2,1)S(1)} %collective-permute-done.15.refs_1_, bf16[16,4096]{1,0:T(8,128)(2,1)S(1)} %collective-permute-done.16.refs_2_, bf16[16,4096]{1,0:T(8,128)(2,1)S(1)} %collective-permute-done.17.refs_3_, ...), custom_call_target="tpu_custom_call" | custom-call | tf_op jit(solution)/shard_map/field/pallas_call | solution.py:583
  (19 shorter events, 0.1 us)
Async XLA Ops:
  0.6 17.0 %copy-start = (bf16[2,16,16,16,128]{4,3,2,1,0:T(8,128)(2,1)S(1)}, bf16[2,16,16,16,128]{4,3,2,1,0:T(8,128)(2,1)}, u32[]{:S(2)}) copy-start(bf16[2,16,16,16,128]{4,3,2,1,0:T(8,128)(2,1)} %weight_ref.3) | copy-start | bytes 6291460
  0.6 27.8 %copy-start.1 = (bf16[16,16]{1,0:T(8,128)(2,1)S(1)}, bf16[16,16]{1,0:T(8,128)(2,1)}, u32[]{:S(2)}) copy-start(bf16[16,16]{1,0:T(8,128)(2,1)} %refs_10_.2) | copy-start | bytes 1540
  0.7 27.8 %copy-start.2 = (f32[16]{0:T(128)S(1)}, f32[16]{0:T(128)}, u32[]{:S(2)}) copy-start(f32[16]{0:T(128)} %param.11) | copy-start | bytes 196
  4.2 2.1 %collective-permute-start = (bf16[64,4096]{1,0:T(8,128)(2,1)S(1)}, bf16[64,4096]{1,0:T(8,128)(2,1)S(1)}, u32[]{:S(2)}, u32[]{:S(2)}) collective-permute-start(bf16[64,4096]{1,0:T(8,128)(2,1)S(1)} %columns.1.mine_ref), channel_id=1, source_target_pairs={{0,1},{1,0},{2,3},{3,2},{4,5},{5,4},{6,7},{7,6},{8,9},{9,8},{10,11... | collective-permute-start | bytes 1572872 | tf_op jit(solution)/shard_map/ppermute | solution.py:375
  6.7 6.9 %collective-permute-start.1 = (bf16[16,4096]{1,0:T(8,128)(2,1)S(1)}, bf16[16,4096]{1,0:T(8,128)(2,1)S(1)}, u32[]{:S(2)}, u32[]{:S(2)}) collective-permute-start(bf16[16,4096]{1,0:T(8,128)(2,1)S(1)} %get-tuple-element.25), channel_id=1, source_target_pairs={{0,2},{1,3},{2,0},{3,1},{4,6},{5,7},{6,4},{7,5},{8,10},{9,11},{10,... | collective-permute-start | bytes 393224 | tf_op jit(solution)/shard_map/ppermute | solution.py:375
  9.6 8.1 %collective-permute-start.2 = (bf16[16,4096]{1,0:T(8,128)(2,1)S(1)}, bf16[16,4096]{1,0:T(8,128)(2,1)S(1)}, u32[]{:S(2)}, u32[]{:S(2)}) collective-permute-start(bf16[16,4096]{1,0:T(8,128)(2,1)S(1)} %get-tuple-element.26), channel_id=1, source_target_pairs={{0,4},{1,5},{2,6},{3,7},{4,0},{5,1},{6,2},{7,3},{8,12},{9,13},{10,... | collective-permute-start | bytes 393224 | tf_op jit(solution)/shard_map/ppermute | solution.py:375
  11.1 6.5 %collective-permute-start.3 = (bf16[16,4096]{1,0:T(8,128)(2,1)S(1)}, bf16[16,4096]{1,0:T(8,128)(2,1)S(1)}, u32[]{:S(2)}, u32[]{:S(2)}) collective-permute-start(bf16[16,4096]{1,0:T(8,128)(2,1)S(1)} %get-tuple-element.27), channel_id=1, source_target_pairs={{0,6},{1,7},{2,4},{3,5},{4,2},{5,3},{6,0},{7,1},{8,14},{9,15},{10,... | collective-permute-start | bytes 393224 | tf_op jit(solution)/shard_map/ppermute | solution.py:375
  18.4 6.0 %collective-permute-start.4 = (bf16[16,4096]{1,0:T(8,128)(2,1)S(1)}, bf16[16,4096]{1,0:T(8,128)(2,1)S(1)}, u32[]{:S(2)}, u32[]{:S(2)}) collective-permute-start(bf16[16,4096]{1,0:T(8,128)(2,1)S(1)} %get-tuple-element.28.refs_0_), channel_id=1, source_target_pairs={{0,2},{1,3},{2,0},{3,1},{4,6},{5,7},{6,4},{7,5},{8,10},{9,11},{10,... | collective-permute-start | bytes 393224 | tf_op jit(solution)/shard_map/ppermute | solution.py:375
  19.7 7.2 %collective-permute-start.5 = (bf16[16,4096]{1,0:T(8,128)(2,1)S(1)}, bf16[16,4096]{1,0:T(8,128)(2,1)S(1)}, u32[]{:S(2)}, u32[]{:S(2)}) collective-permute-start(bf16[16,4096]{1,0:T(8,128)(2,1)S(1)} %get-tuple-element.28.refs_0_), channel_id=1, source_target_pairs={{0,4},{1,5},{2,6},{3,7},{4,0},{5,1},{6,2},{7,3},{8,12},{9,13},{10,... | collective-permute-start | bytes 393224 | tf_op jit(solution)/shard_map/ppermute | solution.py:375
  20.5 6.4 %collective-permute-start.6 = (bf16[16,4096]{1,0:T(8,128)(2,1)S(1)}, bf16[16,4096]{1,0:T(8,128)(2,1)S(1)}, u32[]{:S(2)}, u32[]{:S(2)}) collective-permute-start(bf16[16,4096]{1,0:T(8,128)(2,1)S(1)} %get-tuple-element.28.refs_0_), channel_id=1, source_target_pairs={{0,6},{1,7},{2,4},{3,5},{4,2},{5,3},{6,0},{7,1},{8,14},{9,15},{10,... | collective-permute-start | bytes 393224 | tf_op jit(solution)/shard_map/ppermute | solution.py:375
  22.2 5.5 %collective-permute-start.7 = (bf16[16,4096]{1,0:T(8,128)(2,1)S(1)}, bf16[16,4096]{1,0:T(8,128)(2,1)S(1)}, u32[]{:S(2)}, u32[]{:S(2)}) collective-permute-start(bf16[16,4096]{1,0:T(8,128)(2,1)S(1)} %get-tuple-element.28.refs_0_), channel_id=1, source_target_pairs={{0,1},{1,0},{2,3},{3,2},{4,5},{5,4},{6,7},{7,6},{8,9},{9,8},{10,11... | collective-permute-start | bytes 393224 | tf_op jit(solution)/shard_map/ppermute | solution.py:375
  24.4 3.3 %collective-permute-start.8 = (bf16[16,4096]{1,0:T(8,128)(2,1)S(1)}, bf16[16,4096]{1,0:T(8,128)(2,1)S(1)}, u32[]{:S(2)}, u32[]{:S(2)}) collective-permute-start(bf16[16,4096]{1,0:T(8,128)(2,1)S(1)} %collective-permute-done.4.refs_1_), channel_id=1, source_target_pairs={{0,1},{1,0},{2,3},{3,2},{4,5},{5,4},{6,7},{7,6},{8,9},{9,8},{10,11... | collective-permute-start | bytes 393224 | tf_op jit(solution)/shard_map/ppermute | solution.py:375
  26.9 1.3 %collective-permute-start.9 = (bf16[16,4096]{1,0:T(8,128)(2,1)S(1)}, bf16[16,4096]{1,0:T(8,128)(2,1)S(1)}, u32[]{:S(2)}, u32[]{:S(2)}) collective-permute-start(bf16[16,4096]{1,0:T(8,128)(2,1)S(1)} %collective-permute-done.5.refs_2_), channel_id=1, source_target_pairs={{0,1},{1,0},{2,3},{3,2},{4,5},{5,4},{6,7},{7,6},{8,9},{9,8},{10,11... | collective-permute-start | bytes 393224 | tf_op jit(solution)/shard_map/ppermute | solution.py:375
  26.9 1.5 %collective-permute-start.10 = (bf16[16,4096]{1,0:T(8,128)(2,1)S(1)}, bf16[16,4096]{1,0:T(8,128)(2,1)S(1)}, u32[]{:S(2)}, u32[]{:S(2)}) collective-permute-start(bf16[16,4096]{1,0:T(8,128)(2,1)S(1)} %collective-permute-done.6.refs_3_), channel_id=1, source_target_pairs={{0,1},{1,0},{2,3},{3,2},{4,5},{5,4},{6,7},{7,6},{8,9},{9,8},{10,11... | collective-permute-start | bytes 393224 | tf_op jit(solution)/shard_map/ppermute | solution.py:375
  39.2 1.9 %collective-permute-start.11 = (bf16[64,4224]{1,0:T(8,128)(2,1)S(1)}, bf16[64,4224]{1,0:T(8,128)(2,1)S(1)}, u32[]{:S(2)}, u32[]{:S(2)}) collective-permute-start(bf16[64,4224]{1,0:T(8,128)(2,1)S(1)} %get-tuple-element.29.mine_ref), channel_id=1, source_target_pairs={{0,1},{1,0},{2,3},{3,2},{4,5},{5,4},{6,7},{7,6},{8,9},{9,8},{10,11... | collective-permute-start | bytes 1622024 | tf_op jit(solution)/shard_map/ppermute | solution.py:375
  41.6 7.7 %collective-permute-start.12 = (bf16[16,4224]{1,0:T(8,128)(2,1)S(1)}, bf16[16,4224]{1,0:T(8,128)(2,1)S(1)}, u32[]{:S(2)}, u32[]{:S(2)}) collective-permute-start(bf16[16,4224]{1,0:T(8,128)(2,1)S(1)} %get-tuple-element.31), channel_id=1, source_target_pairs={{0,2},{1,3},{2,0},{3,1},{4,6},{5,7},{6,4},{7,5},{8,10},{9,11},{10,... | collective-permute-start | bytes 405512 | tf_op jit(solution)/shard_map/ppermute | solution.py:375
  42.9 8.4 %collective-permute-start.13 = (bf16[16,4224]{1,0:T(8,128)(2,1)S(1)}, bf16[16,4224]{1,0:T(8,128)(2,1)S(1)}, u32[]{:S(2)}, u32[]{:S(2)}) collective-permute-start(bf16[16,4224]{1,0:T(8,128)(2,1)S(1)} %get-tuple-element.32), channel_id=1, source_target_pairs={{0,4},{1,5},{2,6},{3,7},{4,0},{5,1},{6,2},{7,3},{8,12},{9,13},{10,... | collective-permute-start | bytes 405512 | tf_op jit(solution)/shard_map/ppermute | solution.py:375
  43.8 7.6 %collective-permute-start.14 = (bf16[16,4224]{1,0:T(8,128)(2,1)S(1)}, bf16[16,4224]{1,0:T(8,128)(2,1)S(1)}, u32[]{:S(2)}, u32[]{:S(2)}) collective-permute-start(bf16[16,4224]{1,0:T(8,128)(2,1)S(1)} %get-tuple-element.33), channel_id=1, source_target_pairs={{0,6},{1,7},{2,4},{3,5},{4,2},{5,3},{6,0},{7,1},{8,14},{9,15},{10,... | collective-permute-start | bytes 405512 | tf_op jit(solution)/shard_map/ppermute | solution.py:375
  45.1 10.7 %collective-permute-start.22 = (bf16[16,4096]{1,0:T(8,128)(2,1)S(1)}, bf16[16,4096]{1,0:T(8,128)(2,1)S(1)}, u32[]{:S(2)}, u32[]{:S(2)}) collective-permute-start(bf16[16,4096]{1,0:T(8,128)(2,1)S(1)} %get-tuple-element.36.refs_0_), channel_id=1, source_target_pairs={{0,8},{8,0},{16,24},{24,16},{1,9},{9,1},{17,25},{25,17},{2,10},{10... | collective-permute-start | bytes 393224 | tf_op jit(solution)/shard_map/ppermute | solution.py:375
  46.7 12.7 %collective-permute-start.23 = (bf16[16,4096]{1,0:T(8,128)(2,1)S(1)}, bf16[16,4096]{1,0:T(8,128)(2,1)S(1)}, u32[]{:S(2)}, u32[]{:S(2)}) collective-permute-start(bf16[16,4096]{1,0:T(8,128)(2,1)S(1)} %get-tuple-element.36.refs_0_), channel_id=1, source_target_pairs={{0,16},{8,24},{16,0},{24,8},{1,17},{9,25},{17,1},{25,9},{2,18},{10... | collective-permute-start | bytes 393224 | tf_op jit(solution)/shard_map/ppermute | solution.py:375
  52.2 7.2 %collective-permute-start.15 = (bf16[16,4096]{1,0:T(8,128)(2,1)S(1)}, bf16[16,4096]{1,0:T(8,128)(2,1)S(1)}, u32[]{:S(2)}, u32[]{:S(2)}) collective-permute-start(bf16[16,4096]{1,0:T(8,128)(2,1)S(1)} %get-tuple-element.34.refs_0_), channel_id=1, source_target_pairs={{0,2},{1,3},{2,0},{3,1},{4,6},{5,7},{6,4},{7,5},{8,10},{9,11},{10,... | collective-permute-start | bytes 393224 | tf_op jit(solution)/shard_map/ppermute | solution.py:375
  53.0 7.7 %collective-permute-start.16 = (bf16[16,4096]{1,0:T(8,128)(2,1)S(1)}, bf16[16,4096]{1,0:T(8,128)(2,1)S(1)}, u32[]{:S(2)}, u32[]{:S(2)}) collective-permute-start(bf16[16,4096]{1,0:T(8,128)(2,1)S(1)} %get-tuple-element.34.refs_0_), channel_id=1, source_target_pairs={{0,4},{1,5},{2,6},{3,7},{4,0},{5,1},{6,2},{7,3},{8,12},{9,13},{10,... | collective-permute-start | bytes 393224 | tf_op jit(solution)/shard_map/ppermute | solution.py:375
  54.3 6.4 %collective-permute-start.17 = (bf16[16,4096]{1,0:T(8,128)(2,1)S(1)}, bf16[16,4096]{1,0:T(8,128)(2,1)S(1)}, u32[]{:S(2)}, u32[]{:S(2)}) collective-permute-start(bf16[16,4096]{1,0:T(8,128)(2,1)S(1)} %get-tuple-element.34.refs_0_), channel_id=1, source_target_pairs={{0,6},{1,7},{2,4},{3,5},{4,2},{5,3},{6,0},{7,1},{8,14},{9,15},{10,... | collective-permute-start | bytes 393224 | tf_op jit(solution)/shard_map/ppermute | solution.py:375
  55.8 6.9 %collective-permute-start.24 = (bf16[16,4096]{1,0:T(8,128)(2,1)S(1)}, bf16[16,4096]{1,0:T(8,128)(2,1)S(1)}, u32[]{:S(2)}, u32[]{:S(2)}) collective-permute-start(bf16[16,4096]{1,0:T(8,128)(2,1)S(1)} %get-tuple-element.36.refs_0_), channel_id=1, source_target_pairs={{0,24},{8,16},{16,8},{24,0},{1,25},{9,17},{17,9},{25,1},{2,26},{10... | collective-permute-start | bytes 393224 | tf_op jit(solution)/shard_map/ppermute | solution.py:375
  59.4 19.7 %collective-permute-start.18 = (bf16[16,4096]{1,0:T(8,128)(2,1)S(1)}, bf16[16,4096]{1,0:T(8,128)(2,1)S(1)}, u32[]{:S(2)}, u32[]{:S(2)}) collective-permute-start(bf16[16,4096]{1,0:T(8,128)(2,1)S(1)} %get-tuple-element.34.refs_0_), channel_id=1, source_target_pairs={{0,1},{1,0},{2,3},{3,2},{4,5},{5,4},{6,7},{7,6},{8,9},{9,8},{10,11... | collective-permute-start | bytes 393224 | tf_op jit(solution)/shard_map/ppermute | solution.py:375
  59.4 19.7 %collective-permute-start.19 = (bf16[16,4096]{1,0:T(8,128)(2,1)S(1)}, bf16[16,4096]{1,0:T(8,128)(2,1)S(1)}, u32[]{:S(2)}, u32[]{:S(2)}) collective-permute-start(bf16[16,4096]{1,0:T(8,128)(2,1)S(1)} %collective-permute-done.15.refs_1_), channel_id=1, source_target_pairs={{0,1},{1,0},{2,3},{3,2},{4,5},{5,4},{6,7},{7,6},{8,9},{9,8},{10,11... | collective-permute-start | bytes 393224 | tf_op jit(solution)/shard_map/ppermute | solution.py:375
  60.7 18.4 %collective-permute-start.20 = (bf16[16,4096]{1,0:T(8,128)(2,1)S(1)}, bf16[16,4096]{1,0:T(8,128)(2,1)S(1)}, u32[]{:S(2)}, u32[]{:S(2)}) collective-permute-start(bf16[16,4096]{1,0:T(8,128)(2,1)S(1)} %collective-permute-done.16.refs_2_), channel_id=1, source_target_pairs={{0,1},{1,0},{2,3},{3,2},{4,5},{5,4},{6,7},{7,6},{8,9},{9,8},{10,11... | collective-permute-start | bytes 393224 | tf_op jit(solution)/shard_map/ppermute | solution.py:375
  60.7 18.4 %collective-permute-start.21 = (bf16[16,4096]{1,0:T(8,128)(2,1)S(1)}, bf16[16,4096]{1,0:T(8,128)(2,1)S(1)}, u32[]{:S(2)}, u32[]{:S(2)}) collective-permute-start(bf16[16,4096]{1,0:T(8,128)(2,1)S(1)} %collective-permute-done.17.refs_3_), channel_id=1, source_target_pairs={{0,1},{1,0},{2,3},{3,2},{4,5},{5,4},{6,7},{7,6},{8,9},{9,8},{10,11... | collective-permute-start | bytes 393224 | tf_op jit(solution)/shard_map/ppermute | solution.py:375
  62.6 4.0 %collective-permute-start.25 = (bf16[16,1152]{1,0:T(8,128)(2,1)S(1)}, bf16[16,1152]{1,0:T(8,128)(2,1)S(1)}, u32[]{:S(2)}, u32[]{:S(2)}) collective-permute-start(bf16[16,1152]{1,0:T(8,128)(2,1)S(1)} %get-tuple-element.38), channel_id=1, source_target_pairs={{0,8},{8,0},{16,24},{24,16},{1,9},{9,1},{17,25},{25,17},{2,10},{10... | collective-permute-start | bytes 110600 | tf_op jit(solution)/shard_map/ppermute | solution.py:375
  66.6 5.0 %collective-permute-start.26 = (bf16[16,1152]{1,0:T(8,128)(2,1)S(1)}, bf16[16,1152]{1,0:T(8,128)(2,1)S(1)}, u32[]{:S(2)}, u32[]{:S(2)}) collective-permute-start(bf16[16,1152]{1,0:T(8,128)(2,1)S(1)} %get-tuple-element.39), channel_id=1, source_target_pairs={{0,16},{8,24},{16,0},{24,8},{1,17},{9,25},{17,1},{25,9},{2,18},{10... | collective-permute-start | bytes 110600 | tf_op jit(solution)/shard_map/ppermute | solution.py:375
  71.6 5.8 %collective-permute-start.27 = (bf16[16,1152]{1,0:T(8,128)(2,1)S(1)}, bf16[16,1152]{1,0:T(8,128)(2,1)S(1)}, u32[]{:S(2)}, u32[]{:S(2)}) collective-permute-start(bf16[16,1152]{1,0:T(8,128)(2,1)S(1)} %get-tuple-element.40), channel_id=1, source_target_pairs={{0,24},{8,16},{16,8},{24,0},{1,25},{9,17},{17,9},{25,1},{2,26},{10... | collective-permute-start | bytes 110600 | tf_op jit(solution)/shard_map/ppermute | solution.py:375

commit v2 on v1

--- a/solution.py
+++ b/solution.py
@@ -308,7 +308,7 @@
         mixer[...] = channel_map(local_ref, chans, False)
         total[...] = jnp.zeros_like(total)
         outer[...] = jnp.zeros_like(outer)
-        sums_ref[...] = jnp.zeros_like(sums_ref)
+        sums_ref[:, chans * lanes :] = jnp.zeros((here, sums_ref.shape[1] - chans * lanes), BF16)
 
     mix = mixer[...]
     group = lax.broadcasted_iota(jnp.int32, (size, chans), 0) // GROUP
@@ -323,7 +323,10 @@
         cot = cot_ref[:, block, :].reshape(size, tile)
         grad = cot * gelu_slope(preact.astype(BF16))
         grad_ref[:, block, :] = grad.reshape(chans, GROUP, tile)
-        both = both + dot_nt(field, grad)
+    for at in range(0, here, GROUP):
+        block = slice(at, at + GROUP)
+        field = field_ref[:, block, :].reshape(size, tile)
+        both = both + dot_nt(field, grad_ref[:, block, :].reshape(size, tile))
     outer[...] += both
     total[...] += dot(grad_ref[...].reshape(chans * here, tile), forward_ref[...])
 
@@ -353,7 +356,7 @@
 
 def field_kernel(chans, modes, scale, count, *refs):
     chunks = refs[:count]
-    phase_ref, inverse_ref, local_ref, grad_ref, out_ref, rows, mixer = refs[count:]
+    phase_ref, inverse_ref, local_ref, grad_ref, out_ref, rows, mixer, wide = refs[count:]
     size = chans * GROUP
     here, tile = grad_ref.shape[1:]
 
@@ -363,10 +366,11 @@
         mixer[...] = channel_map(local_ref, chans, True)
 
     mix = mixer[...]
+    wide[...] = dot(rows[...], inverse_ref[...])
     for at in range(0, here, GROUP):
         block = slice(at, at + GROUP)
-        mine = rows[at * chans : (at + GROUP) * chans]
-        value = dot(mix, grad_ref[:, block, :].reshape(size, tile)) + dot(mine, inverse_ref[...])
+        value = dot(mix, grad_ref[:, block, :].reshape(size, tile))
+        value = value + wide[at * chans : (at + GROUP) * chans]
         out_ref[:, block, :] = value.astype(BF16).reshape(chans, GROUP, tile)
 
 
@@ -577,6 +581,7 @@
         scratch_shapes=[
             pltpu.VMEM((chans * rows_here, lanes), BF16),
             pltpu.VMEM((size, size), BF16),
+            pltpu.VMEM((chans * rows_here, block.block_shape[2]), F32),
         ],
         compiler_params=room(20),
     )

time: 85.6 us -> 85.3 us (level)
  no operation moved by 1% of the time
where the time goes in v2:
time: 85.3 us; the launch traced here: 85.1 us
  starting transfers between devices  33.2 us (39%)
  waiting for transfers between devices  25.8 us (30%)
  Pallas kernels  24.4 us (29%)
    ppermute x28, starting transfers between devices, swap(): return lax.ppermute(value, axis, [(at, at ^ mask) for at in range(size)])  33.2 us
    ppermute x28, waiting for transfers between devices, swap(): return lax.ppermute(value, axis, [(at, at ^ mask) for at in range(size)])  25.8 us
    pallas_call x1, Pallas kernels, on_device(): main(*mixed, to_rows, streamed(inverse), streamed(forward), local_weight,...  10.5 us
    pallas_call x1, Pallas kernels, on_device(): final(*freq_grad, to_rows, streamed(inverse), local_weight, streamed(grad...  6.28 us
    pallas_call x1, Pallas kernels, on_device(): pl.pallas_call(columns_kernel, name='columns', grid=(tiles,), in_specs=[b...  3.5 us
  transfers between devices with their start and end apart: 28, of which 14 were waited for; matrix products, arithmetic and copies ran while one was open for 1% of the time, Pallas kernels for 3%

profile of v2, /device:TPU:0, one launch (start us, length us, event | category | flops | bytes accessed | tf_op | source)
XLA Modules:
  0.0 85.1 jit_solution(12680054045469394503)
XLA Ops:
  0.7 3.5 %columns.1.mine_ref = bf16[64,4096]{1,0:T(8,128)(2,1)S(1)} custom-call(bf16[16,64,2048]{2,1,0:T(8,128)(2,1)} %bitcast.7, bf16[2048,256]{1,0:T(8,128)(2,1)} %constant.90.clone.table_ref.refs_10_), custom_call_target="tpu_custom_call" | custom-call | tf_op jit(solution)/shard_map/columns/pallas_call | solution.py:479
  4.2 0.6 collective-permute-start
  4.7 0.1 iota_add_fusion.1
  4.8 0.1 add.131
  4.9 0.1 pad_add_fusion
  5.0 0.2 cosine_convert_fusion.1
  5.2 1.0 %collective-permute-done.other_ref = bf16[64,4096]{1,0:T(8,128)(2,1)S(1)} collective-permute-done((bf16[64,4096]{1,0:T(8,128)(2,1)S(1)}, bf16[64,4096]{1,0:T(8,128)(2,1)S(1)}, u32[]{:S(2)}, u32[]{:S(2)}) %collective-permute-start) | collective-permute-done | bytes 524320 | tf_op jit(solution)/shard_map/ppermute | solution.py:379
  6.3 0.4 rows.2
  6.7 2.9 %collective-permute-start.1 = (bf16[16,4096]{1,0:T(8,128)(2,1)S(1)}, bf16[16,4096]{1,0:T(8,128)(2,1)S(1)}, u32[]{:S(2)}, u32[]{:S(2)}) collective-permute-start(bf16[16,4096]{1,0:T(8,128)(2,1)S(1)} %get-tuple-element.25), channel_id=1, source_target_pairs={{0,2},{1,3},{2,0},{3,1},{4,6},{5,7},{6,4},{7,5},{8,10},{9,11},{10,... | collective-permute-start | bytes 393224 | tf_op jit(solution)/shard_map/ppermute | solution.py:379
  9.6 1.5 %collective-permute-start.2 = (bf16[16,4096]{1,0:T(8,128)(2,1)S(1)}, bf16[16,4096]{1,0:T(8,128)(2,1)S(1)}, u32[]{:S(2)}, u32[]{:S(2)}) collective-permute-start(bf16[16,4096]{1,0:T(8,128)(2,1)S(1)} %get-tuple-element.26), channel_id=1, source_target_pairs={{0,4},{1,5},{2,6},{3,7},{4,0},{5,1},{6,2},{7,3},{8,12},{9,13},{10,... | collective-permute-start | bytes 393224 | tf_op jit(solution)/shard_map/ppermute | solution.py:379
  11.1 0.0 collective-permute-start.3
  11.1 2.4 %collective-permute-done.1.refs_1_ = bf16[16,4096]{1,0:T(8,128)(2,1)S(1)} collective-permute-done((bf16[16,4096]{1,0:T(8,128)(2,1)S(1)}, bf16[16,4096]{1,0:T(8,128)(2,1)S(1)}, u32[]{:S(2)}, u32[]{:S(2)}) %collective-permute-start.1) | collective-permute-done | bytes 131104 | tf_op jit(solution)/shard_map/ppermute | solution.py:379
  13.6 4.1 %collective-permute-done.2.refs_2_ = bf16[16,4096]{1,0:T(8,128)(2,1)S(1)} collective-permute-done((bf16[16,4096]{1,0:T(8,128)(2,1)S(1)}, bf16[16,4096]{1,0:T(8,128)(2,1)S(1)}, u32[]{:S(2)}, u32[]{:S(2)}) %collective-permute-start.2) | collective-permute-done | bytes 131104 | tf_op jit(solution)/shard_map/ppermute | solution.py:379
  17.7 0.0 collective-permute-done.3.refs_3_
  17.7 0.7 mix.1
  18.4 1.3 %collective-permute-start.4 = (bf16[16,4096]{1,0:T(8,128)(2,1)S(1)}, bf16[16,4096]{1,0:T(8,128)(2,1)S(1)}, u32[]{:S(2)}, u32[]{:S(2)}) collective-permute-start(bf16[16,4096]{1,0:T(8,128)(2,1)S(1)} %get-tuple-element.28.refs_0_), channel_id=1, source_target_pairs={{0,2},{1,3},{2,0},{3,1},{4,6},{5,7},{6,4},{7,5},{8,10},{9,11},{10,... | collective-permute-start | bytes 393224 | tf_op jit(solution)/shard_map/ppermute | solution.py:379
  19.7 0.8 collective-permute-start.5
  20.5 1.4 %collective-permute-start.6 = (bf16[16,4096]{1,0:T(8,128)(2,1)S(1)}, bf16[16,4096]{1,0:T(8,128)(2,1)S(1)}, u32[]{:S(2)}, u32[]{:S(2)}) collective-permute-start(bf16[16,4096]{1,0:T(8,128)(2,1)S(1)} %get-tuple-element.28.refs_0_), channel_id=1, source_target_pairs={{0,6},{1,7},{2,4},{3,5},{4,2},{5,3},{6,0},{7,1},{8,14},{9,15},{10,... | collective-permute-start | bytes 393224 | tf_op jit(solution)/shard_map/ppermute | solution.py:379
  22.0 0.1 iota_add_fusion
  22.0 0.1 add.142
  22.1 0.1 and_select_fusion
  22.2 0.0 collective-permute-start.7
  22.2 2.2 %collective-permute-done.4.refs_1_ = bf16[16,4096]{1,0:T(8,128)(2,1)S(1)} collective-permute-done((bf16[16,4096]{1,0:T(8,128)(2,1)S(1)}, bf16[16,4096]{1,0:T(8,128)(2,1)S(1)}, u32[]{:S(2)}, u32[]{:S(2)}) %collective-permute-start.4) | collective-permute-done | bytes 131104 | tf_op jit(solution)/shard_map/ppermute | solution.py:379
  24.4 0.0 collective-permute-start.8
  24.4 2.5 %collective-permute-done.5.refs_2_ = bf16[16,4096]{1,0:T(8,128)(2,1)S(1)} collective-permute-done((bf16[16,4096]{1,0:T(8,128)(2,1)S(1)}, bf16[16,4096]{1,0:T(8,128)(2,1)S(1)}, u32[]{:S(2)}, u32[]{:S(2)}) %collective-permute-start.5) | collective-permute-done | bytes 131104 | tf_op jit(solution)/shard_map/ppermute | solution.py:379
  26.9 0.0 collective-permute-start.9
  26.9 0.0 collective-permute-done.6.refs_3_
  26.9 0.5 collective-permute-start.10
  27.5 0.2 cosine_convert_fusion
  27.7 0.0 collective-permute-done.7.refs_4_
  27.7 0.6 collective-permute-done.9.refs_6_
  28.3 0.2 collective-permute-done.10.refs_7_
  28.5 10.5 %main.1 = (bf16[16,64,2048]{2,1,0:T(8,128)(2,1)}, bf16[64,4224]{1,0:T(8,128)(2,1)S(1)}) custom-call(bf16[16,4096]{1,0:T(8,128)(2,1)S(1)} %get-tuple-element.28.refs_0_, bf16[16,4096]{1,0:T(8,128)(2,1)S(1)} %collective-permute-done.4.refs_1_, bf16[16,4096]{1,0:T(8,128)(2,1)S(1)} %collective-permute-done.5.refs_2_, ...), custom_call_target="tpu_custom_call" | custom-call | tf_op jit(solution)/shard_map/main/pallas_call | solution.py:529
  39.0 0.3 collective-permute-start.11
  39.3 1.6 %collective-permute-done.11.other_ref = bf16[64,4224]{1,0:T(8,128)(2,1)S(1)} collective-permute-done((bf16[64,4224]{1,0:T(8,128)(2,1)S(1)}, bf16[64,4224]{1,0:T(8,128)(2,1)S(1)}, u32[]{:S(2)}, u32[]{:S(2)}) %collective-permute-start.11) | collective-permute-done | bytes 540704 | tf_op jit(solution)/shard_map/ppermute | solution.py:379
  40.9 0.4 rows.3
  41.3 1.4 %collective-permute-start.12 = (bf16[16,4224]{1,0:T(8,128)(2,1)S(1)}, bf16[16,4224]{1,0:T(8,128)(2,1)S(1)}, u32[]{:S(2)}, u32[]{:S(2)}) collective-permute-start(bf16[16,4224]{1,0:T(8,128)(2,1)S(1)} %get-tuple-element.31), channel_id=1, source_target_pairs={{0,2},{1,3},{2,0},{3,1},{4,6},{5,7},{6,4},{7,5},{8,10},{9,11},{10,... | collective-permute-start | bytes 405512 | tf_op jit(solution)/shard_map/ppermute | solution.py:379
  42.7 0.9 %collective-permute-start.13 = (bf16[16,4224]{1,0:T(8,128)(2,1)S(1)}, bf16[16,4224]{1,0:T(8,128)(2,1)S(1)}, u32[]{:S(2)}, u32[]{:S(2)}) collective-permute-start(bf16[16,4224]{1,0:T(8,128)(2,1)S(1)} %get-tuple-element.32), channel_id=1, source_target_pairs={{0,4},{1,5},{2,6},{3,7},{4,0},{5,1},{6,2},{7,3},{8,12},{9,13},{10,... | collective-permute-start | bytes 405512 | tf_op jit(solution)/shard_map/ppermute | solution.py:379
  43.6 1.3 %collective-permute-start.14 = (bf16[16,4224]{1,0:T(8,128)(2,1)S(1)}, bf16[16,4224]{1,0:T(8,128)(2,1)S(1)}, u32[]{:S(2)}, u32[]{:S(2)}) collective-permute-start(bf16[16,4224]{1,0:T(8,128)(2,1)S(1)} %get-tuple-element.33), channel_id=1, source_target_pairs={{0,6},{1,7},{2,4},{3,5},{4,2},{5,3},{6,0},{7,1},{8,14},{9,15},{10,... | collective-permute-start | bytes 405512 | tf_op jit(solution)/shard_map/ppermute | solution.py:379
  44.9 1.6 %collective-permute-start.22 = (bf16[16,4096]{1,0:T(8,128)(2,1)S(1)}, bf16[16,4096]{1,0:T(8,128)(2,1)S(1)}, u32[]{:S(2)}, u32[]{:S(2)}) collective-permute-start(bf16[16,4096]{1,0:T(8,128)(2,1)S(1)} %get-tuple-element.36.refs_0_), channel_id=1, source_target_pairs={{0,8},{8,0},{16,24},{24,16},{1,9},{9,1},{17,25},{25,17},{2,10},{10... | collective-permute-start | bytes 393224 | tf_op jit(solution)/shard_map/ppermute | solution.py:379
  46.5 2.6 %collective-permute-start.23 = (bf16[16,4096]{1,0:T(8,128)(2,1)S(1)}, bf16[16,4096]{1,0:T(8,128)(2,1)S(1)}, u32[]{:S(2)}, u32[]{:S(2)}) collective-permute-start(bf16[16,4096]{1,0:T(8,128)(2,1)S(1)} %get-tuple-element.36.refs_0_), channel_id=1, source_target_pairs={{0,16},{8,24},{16,0},{24,8},{1,17},{9,25},{17,1},{25,9},{2,18},{10... | collective-permute-start | bytes 393224 | tf_op jit(solution)/shard_map/ppermute | solution.py:379
  49.0 2.1 %collective-permute-done.13.refs_2_ = bf16[16,4224]{1,0:T(8,128)(2,1)S(1)} collective-permute-done((bf16[16,4224]{1,0:T(8,128)(2,1)S(1)}, bf16[16,4224]{1,0:T(8,128)(2,1)S(1)}, u32[]{:S(2)}, u32[]{:S(2)}) %collective-permute-start.13) | collective-permute-done | bytes 135200 | tf_op jit(solution)/shard_map/ppermute | solution.py:379
  51.1 0.0 collective-permute-done.14.refs_3_
  51.1 0.8 back.1
  52.0 0.8 collective-permute-start.15
  52.8 1.3 %collective-permute-start.16 = (bf16[16,4096]{1,0:T(8,128)(2,1)S(1)}, bf16[16,4096]{1,0:T(8,128)(2,1)S(1)}, u32[]{:S(2)}, u32[]{:S(2)}) collective-permute-start(bf16[16,4096]{1,0:T(8,128)(2,1)S(1)} %get-tuple-element.34.refs_0_), channel_id=1, source_target_pairs={{0,4},{1,5},{2,6},{3,7},{4,0},{5,1},{6,2},{7,3},{8,12},{9,13},{10,... | collective-permute-start | bytes 393224 | tf_op jit(solution)/shard_map/ppermute | solution.py:379
  54.1 1.4 %collective-permute-start.17 = (bf16[16,4096]{1,0:T(8,128)(2,1)S(1)}, bf16[16,4096]{1,0:T(8,128)(2,1)S(1)}, u32[]{:S(2)}, u32[]{:S(2)}) collective-permute-start(bf16[16,4096]{1,0:T(8,128)(2,1)S(1)} %get-tuple-element.34.refs_0_), channel_id=1, source_target_pairs={{0,6},{1,7},{2,4},{3,5},{4,2},{5,3},{6,0},{7,1},{8,14},{9,15},{10,... | collective-permute-start | bytes 393224 | tf_op jit(solution)/shard_map/ppermute | solution.py:379
  55.5 0.0 collective-permute-done.22.refs_1_
  55.5 3.6 %collective-permute-start.24 = (bf16[16,4096]{1,0:T(8,128)(2,1)S(1)}, bf16[16,4096]{1,0:T(8,128)(2,1)S(1)}, u32[]{:S(2)}, u32[]{:S(2)}) collective-permute-start(bf16[16,4096]{1,0:T(8,128)(2,1)S(1)} %get-tuple-element.36.refs_0_), channel_id=1, source_target_pairs={{0,24},{8,16},{16,8},{24,0},{1,25},{9,17},{17,9},{25,1},{2,26},{10... | collective-permute-start | bytes 393224 | tf_op jit(solution)/shard_map/ppermute | solution.py:379
  59.2 0.0 collective-permute-done.23.refs_2_
  59.2 0.0 collective-permute-start.18
  59.2 0.5 collective-permute-start.19
  59.7 0.8 collective-permute-done.16.refs_2_
  60.5 0.0 collective-permute-start.20
  60.5 0.5 collective-permute-start.21
  61.0 1.4 %collective-permute-done.24.refs_3_ = bf16[16,4096]{1,0:T(8,128)(2,1)S(1)} collective-permute-done((bf16[16,4096]{1,0:T(8,128)(2,1)S(1)}, bf16[16,4096]{1,0:T(8,128)(2,1)S(1)}, u32[]{:S(2)}, u32[]{:S(2)}) %collective-permute-start.24) | collective-permute-done | bytes 131104 | tf_op jit(solution)/shard_map/ppermute | solution.py:379
  62.4 1.3 %collective-permute-start.25 = (bf16[16,1152]{1,0:T(8,128)(2,1)S(1)}, bf16[16,1152]{1,0:T(8,128)(2,1)S(1)}, u32[]{:S(2)}, u32[]{:S(2)}) collective-permute-start(bf16[16,1152]{1,0:T(8,128)(2,1)S(1)} %get-tuple-element.38), channel_id=1, source_target_pairs={{0,8},{8,0},{16,24},{24,16},{1,9},{9,1},{17,25},{25,17},{2,10},{10... | collective-permute-start | bytes 110600 | tf_op jit(solution)/shard_map/ppermute | solution.py:379
  63.7 2.6 %collective-permute-done.25.refs_5_ = bf16[16,1152]{1,0:T(8,128)(2,1)S(1)} collective-permute-done((bf16[16,1152]{1,0:T(8,128)(2,1)S(1)}, bf16[16,1152]{1,0:T(8,128)(2,1)S(1)}, u32[]{:S(2)}, u32[]{:S(2)}) %collective-permute-start.25) | collective-permute-done | bytes 36896 | tf_op jit(solution)/shard_map/ppermute | solution.py:379
  66.4 3.0 %collective-permute-start.26 = (bf16[16,1152]{1,0:T(8,128)(2,1)S(1)}, bf16[16,1152]{1,0:T(8,128)(2,1)S(1)}, u32[]{:S(2)}, u32[]{:S(2)}) collective-permute-start(bf16[16,1152]{1,0:T(8,128)(2,1)S(1)} %get-tuple-element.39), channel_id=1, source_target_pairs={{0,16},{8,24},{16,0},{24,8},{1,17},{9,25},{17,1},{25,9},{2,18},{10... | collective-permute-start | bytes 110600 | tf_op jit(solution)/shard_map/ppermute | solution.py:379
  69.4 1.9 %collective-permute-done.26.refs_6_ = bf16[16,1152]{1,0:T(8,128)(2,1)S(1)} collective-permute-done((bf16[16,1152]{1,0:T(8,128)(2,1)S(1)}, bf16[16,1152]{1,0:T(8,128)(2,1)S(1)}, u32[]{:S(2)}, u32[]{:S(2)}) %collective-permute-start.26) | collective-permute-done | bytes 36896 | tf_op jit(solution)/shard_map/ppermute | solution.py:379
  71.3 3.5 %collective-permute-start.27 = (bf16[16,1152]{1,0:T(8,128)(2,1)S(1)}, bf16[16,1152]{1,0:T(8,128)(2,1)S(1)}, u32[]{:S(2)}, u32[]{:S(2)}) collective-permute-start(bf16[16,1152]{1,0:T(8,128)(2,1)S(1)} %get-tuple-element.40), channel_id=1, source_target_pairs={{0,24},{8,16},{16,8},{24,0},{1,25},{9,17},{17,9},{25,1},{2,26},{10... | collective-permute-start | bytes 110600 | tf_op jit(solution)/shard_map/ppermute | solution.py:379
  74.9 2.2 %collective-permute-done.27.refs_7_ = bf16[16,1152]{1,0:T(8,128)(2,1)S(1)} collective-permute-done((bf16[16,1152]{1,0:T(8,128)(2,1)S(1)}, bf16[16,1152]{1,0:T(8,128)(2,1)S(1)}, u32[]{:S(2)}, u32[]{:S(2)}) %collective-permute-start.27) | collective-permute-done | bytes 36896 | tf_op jit(solution)/shard_map/ppermute | solution.py:379
  77.1 1.7 %weights.1 = (f32[2,16,4,16,128]{4,3,2,1,0:T(8,128)}, f32[16,16]{1,0:T(8,128)}, f32[1,16]{1,0:T(1,128)}) custom-call(bf16[16,4096]{1,0:T(8,128)(2,1)S(1)} %get-tuple-element.36.refs_0_, bf16[16,4096]{1,0:T(8,128)(2,1)S(1)} %collective-permute-done.22.refs_1_, bf16[16,4096]{1,0:T(8,128)(2,1)S(1)} %collective-permute-done.23.refs_2_, ...), custom_call_target="tpu_custom_call" | custom-call | tf_op jit(solution)/shard_map/weights/pallas_call | solution.py:552
  78.8 6.3 %field.1 = bf16[16,64,2048]{2,1,0:T(8,128)(2,1)} custom-call(bf16[16,4096]{1,0:T(8,128)(2,1)S(1)} %get-tuple-element.34.refs_0_, bf16[16,4096]{1,0:T(8,128)(2,1)S(1)} %collective-permute-done.15.refs_1_, bf16[16,4096]{1,0:T(8,128)(2,1)S(1)} %collective-permute-done.16.refs_2_, bf16[16,4096]{1,0:T(8,128)(2,1)S(1)} %collective-permute-done.17.refs_3_, ...), custom_call_target="tpu_custom_call" | custom-call | tf_op jit(solution)/shard_map/field/pallas_call | solution.py:588
  (19 shorter events, 0.1 us)
Async XLA Ops:
  0.6 17.0 %copy-start = (bf16[2,16,16,16,128]{4,3,2,1,0:T(8,128)(2,1)S(1)}, bf16[2,16,16,16,128]{4,3,2,1,0:T(8,128)(2,1)}, u32[]{:S(2)}) copy-start(bf16[2,16,16,16,128]{4,3,2,1,0:T(8,128)(2,1)} %weight_ref.3) | copy-start | bytes 6291460
  0.6 27.8 %copy-start.1 = (bf16[16,16]{1,0:T(8,128)(2,1)S(1)}, bf16[16,16]{1,0:T(8,128)(2,1)}, u32[]{:S(2)}) copy-start(bf16[16,16]{1,0:T(8,128)(2,1)} %refs_10_.2) | copy-start | bytes 1540
  0.7 27.8 %copy-start.2 = (f32[16]{0:T(128)S(1)}, f32[16]{0:T(128)}, u32[]{:S(2)}) copy-start(f32[16]{0:T(128)} %param.11) | copy-start | bytes 196
  4.2 2.1 %collective-permute-start = (bf16[64,4096]{1,0:T(8,128)(2,1)S(1)}, bf16[64,4096]{1,0:T(8,128)(2,1)S(1)}, u32[]{:S(2)}, u32[]{:S(2)}) collective-permute-start(bf16[64,4096]{1,0:T(8,128)(2,1)S(1)} %columns.1.mine_ref), channel_id=1, source_target_pairs={{0,1},{1,0},{2,3},{3,2},{4,5},{5,4},{6,7},{7,6},{8,9},{9,8},{10,11... | collective-permute-start | bytes 1572872 | tf_op jit(solution)/shard_map/ppermute | solution.py:379
  6.7 6.9 %collective-permute-start.1 = (bf16[16,4096]{1,0:T(8,128)(2,1)S(1)}, bf16[16,4096]{1,0:T(8,128)(2,1)S(1)}, u32[]{:S(2)}, u32[]{:S(2)}) collective-permute-start(bf16[16,4096]{1,0:T(8,128)(2,1)S(1)} %get-tuple-element.25), channel_id=1, source_target_pairs={{0,2},{1,3},{2,0},{3,1},{4,6},{5,7},{6,4},{7,5},{8,10},{9,11},{10,... | collective-permute-start | bytes 393224 | tf_op jit(solution)/shard_map/ppermute | solution.py:379
  9.6 8.1 %collective-permute-start.2 = (bf16[16,4096]{1,0:T(8,128)(2,1)S(1)}, bf16[16,4096]{1,0:T(8,128)(2,1)S(1)}, u32[]{:S(2)}, u32[]{:S(2)}) collective-permute-start(bf16[16,4096]{1,0:T(8,128)(2,1)S(1)} %get-tuple-element.26), channel_id=1, source_target_pairs={{0,4},{1,5},{2,6},{3,7},{4,0},{5,1},{6,2},{7,3},{8,12},{9,13},{10,... | collective-permute-start | bytes 393224 | tf_op jit(solution)/shard_map/ppermute | solution.py:379
  11.1 6.5 %collective-permute-start.3 = (bf16[16,4096]{1,0:T(8,128)(2,1)S(1)}, bf16[16,4096]{1,0:T(8,128)(2,1)S(1)}, u32[]{:S(2)}, u32[]{:S(2)}) collective-permute-start(bf16[16,4096]{1,0:T(8,128)(2,1)S(1)} %get-tuple-element.27), channel_id=1, source_target_pairs={{0,6},{1,7},{2,4},{3,5},{4,2},{5,3},{6,0},{7,1},{8,14},{9,15},{10,... | collective-permute-start | bytes 393224 | tf_op jit(solution)/shard_map/ppermute | solution.py:379
  18.4 6.0 %collective-permute-start.4 = (bf16[16,4096]{1,0:T(8,128)(2,1)S(1)}, bf16[16,4096]{1,0:T(8,128)(2,1)S(1)}, u32[]{:S(2)}, u32[]{:S(2)}) collective-permute-start(bf16[16,4096]{1,0:T(8,128)(2,1)S(1)} %get-tuple-element.28.refs_0_), channel_id=1, source_target_pairs={{0,2},{1,3},{2,0},{3,1},{4,6},{5,7},{6,4},{7,5},{8,10},{9,11},{10,... | collective-permute-start | bytes 393224 | tf_op jit(solution)/shard_map/ppermute | solution.py:379
  19.7 7.2 %collective-permute-start.5 = (bf16[16,4096]{1,0:T(8,128)(2,1)S(1)}, bf16[16,4096]{1,0:T(8,128)(2,1)S(1)}, u32[]{:S(2)}, u32[]{:S(2)}) collective-permute-start(bf16[16,4096]{1,0:T(8,128)(2,1)S(1)} %get-tuple-element.28.refs_0_), channel_id=1, source_target_pairs={{0,4},{1,5},{2,6},{3,7},{4,0},{5,1},{6,2},{7,3},{8,12},{9,13},{10,... | collective-permute-start | bytes 393224 | tf_op jit(solution)/shard_map/ppermute | solution.py:379
  20.5 6.4 %collective-permute-start.6 = (bf16[16,4096]{1,0:T(8,128)(2,1)S(1)}, bf16[16,4096]{1,0:T(8,128)(2,1)S(1)}, u32[]{:S(2)}, u32[]{:S(2)}) collective-permute-start(bf16[16,4096]{1,0:T(8,128)(2,1)S(1)} %get-tuple-element.28.refs_0_), channel_id=1, source_target_pairs={{0,6},{1,7},{2,4},{3,5},{4,2},{5,3},{6,0},{7,1},{8,14},{9,15},{10,... | collective-permute-start | bytes 393224 | tf_op jit(solution)/shard_map/ppermute | solution.py:379
  22.2 5.5 %collective-permute-start.7 = (bf16[16,4096]{1,0:T(8,128)(2,1)S(1)}, bf16[16,4096]{1,0:T(8,128)(2,1)S(1)}, u32[]{:S(2)}, u32[]{:S(2)}) collective-permute-start(bf16[16,4096]{1,0:T(8,128)(2,1)S(1)} %get-tuple-element.28.refs_0_), channel_id=1, source_target_pairs={{0,1},{1,0},{2,3},{3,2},{4,5},{5,4},{6,7},{7,6},{8,9},{9,8},{10,11... | collective-permute-start | bytes 393224 | tf_op jit(solution)/shard_map/ppermute | solution.py:379
  24.4 3.3 %collective-permute-start.8 = (bf16[16,4096]{1,0:T(8,128)(2,1)S(1)}, bf16[16,4096]{1,0:T(8,128)(2,1)S(1)}, u32[]{:S(2)}, u32[]{:S(2)}) collective-permute-start(bf16[16,4096]{1,0:T(8,128)(2,1)S(1)} %collective-permute-done.4.refs_1_), channel_id=1, source_target_pairs={{0,1},{1,0},{2,3},{3,2},{4,5},{5,4},{6,7},{7,6},{8,9},{9,8},{10,11... | collective-permute-start | bytes 393224 | tf_op jit(solution)/shard_map/ppermute | solution.py:379
  26.9 1.3 %collective-permute-start.9 = (bf16[16,4096]{1,0:T(8,128)(2,1)S(1)}, bf16[16,4096]{1,0:T(8,128)(2,1)S(1)}, u32[]{:S(2)}, u32[]{:S(2)}) collective-permute-start(bf16[16,4096]{1,0:T(8,128)(2,1)S(1)} %collective-permute-done.5.refs_2_), channel_id=1, source_target_pairs={{0,1},{1,0},{2,3},{3,2},{4,5},{5,4},{6,7},{7,6},{8,9},{9,8},{10,11... | collective-permute-start | bytes 393224 | tf_op jit(solution)/shard_map/ppermute | solution.py:379
  26.9 1.5 %collective-permute-start.10 = (bf16[16,4096]{1,0:T(8,128)(2,1)S(1)}, bf16[16,4096]{1,0:T(8,128)(2,1)S(1)}, u32[]{:S(2)}, u32[]{:S(2)}) collective-permute-start(bf16[16,4096]{1,0:T(8,128)(2,1)S(1)} %collective-permute-done.6.refs_3_), channel_id=1, source_target_pairs={{0,1},{1,0},{2,3},{3,2},{4,5},{5,4},{6,7},{7,6},{8,9},{9,8},{10,11... | collective-permute-start | bytes 393224 | tf_op jit(solution)/shard_map/ppermute | solution.py:379
  39.0 1.9 %collective-permute-start.11 = (bf16[64,4224]{1,0:T(8,128)(2,1)S(1)}, bf16[64,4224]{1,0:T(8,128)(2,1)S(1)}, u32[]{:S(2)}, u32[]{:S(2)}) collective-permute-start(bf16[64,4224]{1,0:T(8,128)(2,1)S(1)} %get-tuple-element.29.mine_ref), channel_id=1, source_target_pairs={{0,1},{1,0},{2,3},{3,2},{4,5},{5,4},{6,7},{7,6},{8,9},{9,8},{10,11... | collective-permute-start | bytes 1622024 | tf_op jit(solution)/shard_map/ppermute | solution.py:379
  41.3 7.7 %collective-permute-start.12 = (bf16[16,4224]{1,0:T(8,128)(2,1)S(1)}, bf16[16,4224]{1,0:T(8,128)(2,1)S(1)}, u32[]{:S(2)}, u32[]{:S(2)}) collective-permute-start(bf16[16,4224]{1,0:T(8,128)(2,1)S(1)} %get-tuple-element.31), channel_id=1, source_target_pairs={{0,2},{1,3},{2,0},{3,1},{4,6},{5,7},{6,4},{7,5},{8,10},{9,11},{10,... | collective-permute-start | bytes 405512 | tf_op jit(solution)/shard_map/ppermute | solution.py:379
  42.7 8.4 %collective-permute-start.13 = (bf16[16,4224]{1,0:T(8,128)(2,1)S(1)}, bf16[16,4224]{1,0:T(8,128)(2,1)S(1)}, u32[]{:S(2)}, u32[]{:S(2)}) collective-permute-start(bf16[16,4224]{1,0:T(8,128)(2,1)S(1)} %get-tuple-element.32), channel_id=1, source_target_pairs={{0,4},{1,5},{2,6},{3,7},{4,0},{5,1},{6,2},{7,3},{8,12},{9,13},{10,... | collective-permute-start | bytes 405512 | tf_op jit(solution)/shard_map/ppermute | solution.py:379
  43.6 7.5 %collective-permute-start.14 = (bf16[16,4224]{1,0:T(8,128)(2,1)S(1)}, bf16[16,4224]{1,0:T(8,128)(2,1)S(1)}, u32[]{:S(2)}, u32[]{:S(2)}) collective-permute-start(bf16[16,4224]{1,0:T(8,128)(2,1)S(1)} %get-tuple-element.33), channel_id=1, source_target_pairs={{0,6},{1,7},{2,4},{3,5},{4,2},{5,3},{6,0},{7,1},{8,14},{9,15},{10,... | collective-permute-start | bytes 405512 | tf_op jit(solution)/shard_map/ppermute | solution.py:379
  44.9 10.7 %collective-permute-start.22 = (bf16[16,4096]{1,0:T(8,128)(2,1)S(1)}, bf16[16,4096]{1,0:T(8,128)(2,1)S(1)}, u32[]{:S(2)}, u32[]{:S(2)}) collective-permute-start(bf16[16,4096]{1,0:T(8,128)(2,1)S(1)} %get-tuple-element.36.refs_0_), channel_id=1, source_target_pairs={{0,8},{8,0},{16,24},{24,16},{1,9},{9,1},{17,25},{25,17},{2,10},{10... | collective-permute-start | bytes 393224 | tf_op jit(solution)/shard_map/ppermute | solution.py:379
  46.5 12.7 %collective-permute-start.23 = (bf16[16,4096]{1,0:T(8,128)(2,1)S(1)}, bf16[16,4096]{1,0:T(8,128)(2,1)S(1)}, u32[]{:S(2)}, u32[]{:S(2)}) collective-permute-start(bf16[16,4096]{1,0:T(8,128)(2,1)S(1)} %get-tuple-element.36.refs_0_), channel_id=1, source_target_pairs={{0,16},{8,24},{16,0},{24,8},{1,17},{9,25},{17,1},{25,9},{2,18},{10... | collective-permute-start | bytes 393224 | tf_op jit(solution)/shard_map/ppermute | solution.py:379
  52.0 7.2 %collective-permute-start.15 = (bf16[16,4096]{1,0:T(8,128)(2,1)S(1)}, bf16[16,4096]{1,0:T(8,128)(2,1)S(1)}, u32[]{:S(2)}, u32[]{:S(2)}) collective-permute-start(bf16[16,4096]{1,0:T(8,128)(2,1)S(1)} %get-tuple-element.34.refs_0_), channel_id=1, source_target_pairs={{0,2},{1,3},{2,0},{3,1},{4,6},{5,7},{6,4},{7,5},{8,10},{9,11},{10,... | collective-permute-start | bytes 393224 | tf_op jit(solution)/shard_map/ppermute | solution.py:379
  52.8 7.7 %collective-permute-start.16 = (bf16[16,4096]{1,0:T(8,128)(2,1)S(1)}, bf16[16,4096]{1,0:T(8,128)(2,1)S(1)}, u32[]{:S(2)}, u32[]{:S(2)}) collective-permute-start(bf16[16,4096]{1,0:T(8,128)(2,1)S(1)} %get-tuple-element.34.refs_0_), channel_id=1, source_target_pairs={{0,4},{1,5},{2,6},{3,7},{4,0},{5,1},{6,2},{7,3},{8,12},{9,13},{10,... | collective-permute-start | bytes 393224 | tf_op jit(solution)/shard_map/ppermute | solution.py:379
  54.1 6.4 %collective-permute-start.17 = (bf16[16,4096]{1,0:T(8,128)(2,1)S(1)}, bf16[16,4096]{1,0:T(8,128)(2,1)S(1)}, u32[]{:S(2)}, u32[]{:S(2)}) collective-permute-start(bf16[16,4096]{1,0:T(8,128)(2,1)S(1)} %get-tuple-element.34.refs_0_), channel_id=1, source_target_pairs={{0,6},{1,7},{2,4},{3,5},{4,2},{5,3},{6,0},{7,1},{8,14},{9,15},{10,... | collective-permute-start | bytes 393224 | tf_op jit(solution)/shard_map/ppermute | solution.py:379
  55.5 6.9 %collective-permute-start.24 = (bf16[16,4096]{1,0:T(8,128)(2,1)S(1)}, bf16[16,4096]{1,0:T(8,128)(2,1)S(1)}, u32[]{:S(2)}, u32[]{:S(2)}) collective-permute-start(bf16[16,4096]{1,0:T(8,128)(2,1)S(1)} %get-tuple-element.36.refs_0_), channel_id=1, source_target_pairs={{0,24},{8,16},{16,8},{24,0},{1,25},{9,17},{17,9},{25,1},{2,26},{10... | collective-permute-start | bytes 393224 | tf_op jit(solution)/shard_map/ppermute | solution.py:379
  59.2 19.6 %collective-permute-start.18 = (bf16[16,4096]{1,0:T(8,128)(2,1)S(1)}, bf16[16,4096]{1,0:T(8,128)(2,1)S(1)}, u32[]{:S(2)}, u32[]{:S(2)}) collective-permute-start(bf16[16,4096]{1,0:T(8,128)(2,1)S(1)} %get-tuple-element.34.refs_0_), channel_id=1, source_target_pairs={{0,1},{1,0},{2,3},{3,2},{4,5},{5,4},{6,7},{7,6},{8,9},{9,8},{10,11... | collective-permute-start | bytes 393224 | tf_op jit(solution)/shard_map/ppermute | solution.py:379
  59.2 19.6 %collective-permute-start.19 = (bf16[16,4096]{1,0:T(8,128)(2,1)S(1)}, bf16[16,4096]{1,0:T(8,128)(2,1)S(1)}, u32[]{:S(2)}, u32[]{:S(2)}) collective-permute-start(bf16[16,4096]{1,0:T(8,128)(2,1)S(1)} %collective-permute-done.15.refs_1_), channel_id=1, source_target_pairs={{0,1},{1,0},{2,3},{3,2},{4,5},{5,4},{6,7},{7,6},{8,9},{9,8},{10,11... | collective-permute-start | bytes 393224 | tf_op jit(solution)/shard_map/ppermute | solution.py:379
  60.5 18.3 %collective-permute-start.20 = (bf16[16,4096]{1,0:T(8,128)(2,1)S(1)}, bf16[16,4096]{1,0:T(8,128)(2,1)S(1)}, u32[]{:S(2)}, u32[]{:S(2)}) collective-permute-start(bf16[16,4096]{1,0:T(8,128)(2,1)S(1)} %collective-permute-done.16.refs_2_), channel_id=1, source_target_pairs={{0,1},{1,0},{2,3},{3,2},{4,5},{5,4},{6,7},{7,6},{8,9},{9,8},{10,11... | collective-permute-start | bytes 393224 | tf_op jit(solution)/shard_map/ppermute | solution.py:379
  60.5 18.3 %collective-permute-start.21 = (bf16[16,4096]{1,0:T(8,128)(2,1)S(1)}, bf16[16,4096]{1,0:T(8,128)(2,1)S(1)}, u32[]{:S(2)}, u32[]{:S(2)}) collective-permute-start(bf16[16,4096]{1,0:T(8,128)(2,1)S(1)} %collective-permute-done.17.refs_3_), channel_id=1, source_target_pairs={{0,1},{1,0},{2,3},{3,2},{4,5},{5,4},{6,7},{7,6},{8,9},{9,8},{10,11... | collective-permute-start | bytes 393224 | tf_op jit(solution)/shard_map/ppermute | solution.py:379
  62.4 4.0 %collective-permute-start.25 = (bf16[16,1152]{1,0:T(8,128)(2,1)S(1)}, bf16[16,1152]{1,0:T(8,128)(2,1)S(1)}, u32[]{:S(2)}, u32[]{:S(2)}) collective-permute-start(bf16[16,1152]{1,0:T(8,128)(2,1)S(1)} %get-tuple-element.38), channel_id=1, source_target_pairs={{0,8},{8,0},{16,24},{24,16},{1,9},{9,1},{17,25},{25,17},{2,10},{10... | collective-permute-start | bytes 110600 | tf_op jit(solution)/shard_map/ppermute | solution.py:379
  66.4 5.0 %collective-permute-start.26 = (bf16[16,1152]{1,0:T(8,128)(2,1)S(1)}, bf16[16,1152]{1,0:T(8,128)(2,1)S(1)}, u32[]{:S(2)}, u32[]{:S(2)}) collective-permute-start(bf16[16,1152]{1,0:T(8,128)(2,1)S(1)} %get-tuple-element.39), channel_id=1, source_target_pairs={{0,16},{8,24},{16,0},{24,8},{1,17},{9,25},{17,1},{25,9},{2,18},{10... | collective-permute-start | bytes 110600 | tf_op jit(solution)/shard_map/ppermute | solution.py:379
  71.3 5.8 %collective-permute-start.27 = (bf16[16,1152]{1,0:T(8,128)(2,1)S(1)}, bf16[16,1152]{1,0:T(8,128)(2,1)S(1)}, u32[]{:S(2)}, u32[]{:S(2)}) collective-permute-start(bf16[16,1152]{1,0:T(8,128)(2,1)S(1)} %get-tuple-element.40), channel_id=1, source_target_pairs={{0,24},{8,16},{16,8},{24,0},{1,25},{9,17},{17,9},{25,1},{2,26},{10... | collective-permute-start | bytes 110600 | tf_op jit(solution)/shard_map/ppermute | solution.py:379
